TPU v7x, 32 devices: a whole 2x2x4 slice. The times are simulated.
32 devices in a mesh: wa: 16 (over z, y, core), ha: 2 (over x).
Axes of the slice: x: 2, y: 2, z: 4, core: 2. Of those that a mesh axis runs over, the one named last changes fastest.
Arguments:
- tokens: bfloat16 [16384, 4096], P('wa'), may hold values from -6 to 6
- expert_ids: int32 [16384, 8], P('wa'), may hold values from 0 to 127, as said below
- keep_mask: int32 [16384, 8], P('wa'), may hold values from 0 to 1, as said below
- route_weight: float32 [16384, 8], P('wa'), may hold values from 0.2 to 1
- gate_weight: bfloat16 [4096, 1536], P('wa', 'ha'), may hold values from -0.09375 to 0.09375
- up_weight: bfloat16 [4096, 1536], P('wa', 'ha'), may hold values from -0.09375 to 0.09375
- down_weight: bfloat16 [4096, 1536], P('wa', 'ha'), may hold values from -0.15625 to 0.15625
Outputs:
- mixed: bfloat16 [16384, 4096], P('wa', 'ha')
Inputs may be any that keep to these rules, and one draw needn't show every extreme that they name: `expert_ids`: each row names 8 different experts. keep_mask[t, k] is 1 exactly where fewer than 128 earlier tokens of the same block of 1024 rows name expert_ids[t, k]; in some block 128 tokens naming expert 0 are kept.
All inputs are finite; a program needn't handle non-finite values.
Results may differ from a plain program's by a relative error of at most 0.005.
Values may be sent and summed in bfloat16 or wider, within the bound.
A program may use at most 128 MiB of HBM per device.

v0:
```python
import functools

import jax
import jax.numpy as jnp
from jax import lax
from jax.experimental import pallas as pl
from jax.experimental.pallas import tpu as pltpu
from jax.sharding import PartitionSpec as P

CAP = 128
TOK_COLS = 512
MESH = pl.DeviceIdType.MESH


def expert_kernel(
    n,
    pos_ref, tok_ref, gate_ref, up_ref, down_ref,
    y_ref,
    w, wd, count, counts, slots, guest, tok_buf, part_out, part_in, gate_acc, up_acc, hidden, own, sent, got,
    load_sem, tok_sem, c_send, c_recv, r_send, r_recv, d_send, d_recv, rd_send, rd_recv, dd_send, dd_recv,
    o_send, o_recv, g_send, g_recv, h_send, h_recv, p_send, p_recv, x_send, x_recv,
):
    side = n // 2
    me = lax.axis_index("wa")
    ha = lax.axis_index("ha")
    core = lax.rem(me, 2)
    half = me // side
    sibling = me + 1 - 2 * core
    across = lax.rem(me + side, n)

    def remote(ref, dst, send, recv, **where):
        return pltpu.make_async_remote_copy(
            src_ref=ref, dst_ref=dst, send_sem=send, recv_sem=recv, device_id=where, device_id_type=MESH
        )

    class Ring:
        def __init__(self, members, base, ref_of, sems):
            self.chips, self.base, self.ref_of = members // 2, base, ref_of
            self.steps = self.chips // 2
            self.r_send, self.r_recv, self.d_send, self.d_recv = sems
            chip = (me - base) // 2
            odd = lax.rem(chip, 2)
            self.place = (1 - odd) * (chip // 2) + odd * (self.chips - 1 - chip // 2)
            self.to = (base + self.at(self.place + 1), base + self.at(self.place - 1))

        def at(self, p):
            p = lax.rem(p + 2 * self.chips, self.chips)
            back = p // self.steps
            return 2 * ((1 - back) * 2 * p + back * (2 * (self.chips - 1 - p) + 1)) + core

        def origin(self, direction, step):
            return self.at(self.place - step) if direction == 0 else self.at(self.place + step)

        def _hop(self, ref, direction, step, k):
            return remote(
                ref, ref, self.r_send.at[direction, step - 1, k], self.r_recv.at[direction, step - 1, k],
                wa=self.to[direction],
            )

        def _pass(self, ref, direction, step, k):
            return remote(
                ref, ref, self.d_send.at[direction, step - 1, k], self.d_recv.at[direction, step - 1, k], wa=sibling
            )

        def send(self, direction, step, k):
            return self._hop(self.ref_of(self.origin(direction, step - 1), k), direction, step, k)

        def recv(self, direction, step, k):
            return self._hop(self.ref_of(self.origin(direction, step), k), direction, step, k)

        def pass_on(self, direction, step, k):
            return self._pass(self.ref_of(self.origin(direction, step), k), direction, step, k)

        def passed(self, direction, step, k):
            index = self.origin(direction, step) + 1 - 2 * core
            return self._pass(self.ref_of(index, k), direction, step, k)

        def serve(self, step, streams, last_forward):
            for k in streams:
                for direction in (0, 1):
                    self.recv(direction, step, k).wait_recv()
                    if not last_forward or k % 2 == direction:
                        self.send(direction, step + 1, k).start()
                    self.pass_on(direction, step, k).start()

        def serve_end(self, streams):
            for k in streams:
                self.recv(k % 2, self.steps, k).wait_recv()
                self.pass_on(k % 2, self.steps, k).start()

        def drain(self, streams):
            @pl.loop(1, self.steps)
            def _(step):
                for k in streams:
                    for direction in (0, 1):
                        self.send(direction, step, k).wait_send()
                        self.pass_on(direction, step, k).wait_send()

            for k in streams:
                self.send(k % 2, self.steps, k).wait_send()
                self.pass_on(k % 2, self.steps, k).wait_send()

    near = Ring(side, half * side, lambda i, k: w.at[k // 2, i, k % 2], (r_send, r_recv, d_send, d_recv))
    full = Ring(n, 0, lambda i, k: wd.at[i, k], (rd_send, rd_recv, dd_send, dd_recv))
    mine = me - half * side
    early, late = (0, 1, 2, 3), (0, 1)

    def own_pass(t, index):
        ref = wd.at[index] if t == 2 else w.at[t, index - half * side]
        return remote(ref, ref, o_send.at[t], o_recv.at[t], wa=sibling)

    def count_copy(k):
        return remote(count, counts.at[me], c_send.at[k], c_recv.at[k], wa=lax.rem(me + k, n))

    def count_got(k):
        return remote(count, counts.at[lax.rem(me - k + n, n)], c_send.at[k], c_recv.at[k], wa=lax.rem(me + k, n))

    def swap(j):
        return remote(sent.at[j], got.at[j], x_send.at[j], x_recv.at[j], ha=1 - ha)

    loads = [
        pltpu.make_async_copy(gate_ref, w.at[0, mine], load_sem.at[0]),
        pltpu.make_async_copy(up_ref, w.at[1, mine], load_sem.at[1]),
        pltpu.make_async_copy(down_ref, wd.at[me], load_sem.at[2]),
    ]
    for load in loads:
        load.start()
    quarter = slots.shape[2]
    per_quarter = quarter // TOK_COLS
    leaving = 2 * (1 - half) + ha
    wanted = (leaving, 2 * half, 2 * half + 1)
    blocks = len(wanted) * per_quarter

    def tok_load(i):
        start = wanted[i // per_quarter] * quarter + i % per_quarter * TOK_COLS
        return pltpu.make_async_copy(
            tok_ref.at[:, pl.ds(pl.multiple_of(start, TOK_COLS), TOK_COLS)], tok_buf.at[i % 2], tok_sem.at[i % 2]
        )

    tok_load(0).start()
    tok_load(1).start()
    place = pos_ref[...]
    chosen = jnp.sum(jnp.where(place >= 0, 1, 0), axis=1, keepdims=True)
    count[...] = jnp.broadcast_to(chosen, count.shape)

    barrier = pltpu.get_barrier_semaphore()

    @pl.loop(1, n)
    def _(k):
        pl.semaphore_signal(barrier, inc=1, device_id={"wa": lax.rem(me + k, n)}, device_id_type=MESH)

    pl.semaphore_signal(barrier, inc=1, device_id={"ha": 1 - ha}, device_id_type=MESH)
    pl.semaphore_wait(barrier, n)

    for t in range(2):
        loads[t].wait()
        for k in (2 * t, 2 * t + 1):
            for direction in (0, 1):
                near.send(direction, 1, k).start()
        own_pass(t, me).start()
    loads[2].wait()
    own_pass(2, me).start()

    slot_ids = lax.broadcasted_iota(jnp.int32, (CAP, pos_ref.shape[1]), 0)
    table = jnp.where(place == slot_ids, jnp.float32(1.0), jnp.float32(0.0)).astype(jnp.bfloat16)
    guest_out = remote(slots.at[0], guest.at[ha], g_send, g_recv, wa=across)
    guest_in = guest_out
    share = remote(guest.at[ha], guest.at[ha], h_send, h_recv, ha=1 - ha)
    shared = remote(guest.at[1 - ha], guest.at[1 - ha], h_send, h_recv, ha=1 - ha)
    for i in range(blocks):
        tok_load(i).wait()
        slots[i // per_quarter, :, i % per_quarter * TOK_COLS:(i % per_quarter + 1) * TOK_COLS] = jnp.dot(
            table, tok_buf[i % 2], preferred_element_type=jnp.float32
        ).astype(jnp.bfloat16)
        if i + 2 < blocks:
            tok_load(i + 2).start()
        if i == per_quarter:
            guest_out.start()

    @pl.loop(1, n)
    def _(k):
        count_copy(k).start()

    @pl.loop(1, near.steps - 1)
    def _(step):
        near.serve(step, early, False)

    near.serve(near.steps - 1, early, True)
    guest_in.wait_recv()
    share.start()
    for k in late:
        for direction in (0, 1):
            full.send(direction, 1, k).start()
    near.serve_end(early)
    for t in (0, 1):
        own_pass(t, sibling).wait_recv()

    @pl.loop(1, near.steps)
    def _(step):
        for k in early:
            for direction in (0, 1):
                near.passed(direction, step, k).wait_recv()

    for k in early:
        near.passed(k % 2, near.steps, k).wait_recv()
    shared.wait_recv()

    hid = w.shape[4]
    group = side // 2

    def project(rows, t):
        total = None
        for q in (0, 1):
            block = w[t, q * group:(q + 1) * group].reshape(quarter, hid)
            term = jnp.dot(rows[q], block, preferred_element_type=jnp.float32)
            total = term if total is None else total + term
        return total

    def partial(t):
        return remote(part_out.at[t], part_in.at[t], p_send.at[t], p_recv.at[t], wa=across)

    part_out[0] = project((guest[0], guest[1]), 0).astype(jnp.bfloat16)
    part_out[1] = project((guest[0], guest[1]), 1).astype(jnp.bfloat16)
    partial(0).start()
    partial(1).start()
    gate_acc[...] = project((slots[1], slots[2]), 0)
    up_acc[...] = project((slots[1], slots[2]), 1)

    ahead = full.steps // 2

    @pl.loop(1, ahead + 1)
    def _(step):
        full.serve(step, late, False)

    partial(0).wait_recv()
    partial(1).wait_recv()
    gate = gate_acc[...] + part_in[0].astype(jnp.float32)
    up = up_acc[...] + part_in[1].astype(jnp.float32)
    hidden[...] = (gate / (1.0 + jnp.exp(-gate)) * up).astype(jnp.bfloat16)
    fd = wd.shape[1] * wd.shape[2]

    def finish(index):
        part = lax.dot_general(
            hidden[...], wd[index].reshape(fd, hid), (((1,), (1,)), ((), ())),
            preferred_element_type=jnp.float32,
        )
        j = lax.rem(index, side)

        @pl.when(index // side == ha)
        def _():
            own[j] = part

        @pl.when(index // side != ha)
        def _():
            sent[j] = part.astype(jnp.bfloat16)
            swap(j).start()

    finish(me)
    own_pass(2, sibling).wait_recv()
    finish(sibling)

    def down_step(step):
        for direction in (0, 1):
            index = full.origin(direction, step)
            finish(index)
            for k in late:
                full.passed(direction, step, k).wait_recv()
            finish(index + 1 - 2 * core)

    @pl.loop(1, ahead + 1)
    def _(step):
        down_step(step)

    @pl.loop(ahead + 1, full.steps - 1)
    def _(step):
        full.serve(step, late, False)
        down_step(step)

    full.serve(full.steps - 1, late, True)
    down_step(full.steps - 1)
    full.serve_end(late)
    far = full.origin(0, full.steps)
    finish(far)
    for k in late:
        full.passed(k % 2, full.steps, k).wait_recv()
    finish(far + 1 - 2 * core)

    @pl.loop(1, n)
    def _(k):
        count_got(k).wait_recv()

    counts[me] = jnp.zeros(counts.shape[1:], jnp.int32)

    def add_count(i, total):
        return total + jnp.where(i < me, counts[i], 0)

    earlier = lax.fori_loop(0, n, add_count, jnp.zeros(counts.shape[1:], jnp.int32))
    slot = lax.broadcasted_iota(jnp.int32, (CAP, fd), 0)
    admitted = slot + earlier[0:1, 0:1] < side * CAP

    for j in range(side):
        swap(j).wait_recv()
        y = jnp.where(admitted, own[j] + got[j].astype(jnp.float32), jnp.float32(0.0))
        high = y.astype(jnp.bfloat16)
        y_ref[0:CAP, j * fd:(j + 1) * fd] = high
        y_ref[CAP:2 * CAP, j * fd:(j + 1) * fd] = (y - high.astype(jnp.float32)).astype(jnp.bfloat16)

    @pl.loop(1, n)
    def _(k):
        count_copy(k).wait_send()

    for t in range(3):
        own_pass(t, me).wait_send()
    guest_out.wait_send()
    share.wait_send()
    partial(0).wait_send()
    partial(1).wait_send()
    near.drain(early)
    full.drain(late)

    @pl.loop(0, side)
    def _(j):
        swap(j).wait_send()


def expert(pos, tokens, gate, up, down):
    n = lax.axis_size("wa")
    fd, hid = gate.shape
    half = fd // 2
    side = n // 2
    quarter = tokens.shape[1] // 4
    any_spec = pl.BlockSpec(memory_space=pl.ANY)
    vmem = pl.BlockSpec(memory_space=pltpu.VMEM)
    dma = pltpu.SemaphoreType.DMA
    return pl.pallas_call(
        functools.partial(expert_kernel, n),
        out_shape=jax.ShapeDtypeStruct((2 * CAP, side * fd), jnp.bfloat16),
        in_specs=[vmem, any_spec, any_spec, any_spec, any_spec],
        out_specs=vmem,
        scratch_shapes=[
            pltpu.VMEM((2, side, 2, half, hid), jnp.bfloat16),
            pltpu.VMEM((n, 2, half, hid), jnp.bfloat16),
            pltpu.VMEM((8, 128), jnp.int32),
            pltpu.VMEM((n, 8, 128), jnp.int32),
            pltpu.VMEM((3, CAP, quarter), jnp.bfloat16),
            pltpu.VMEM((2, CAP, quarter), jnp.bfloat16),
            pltpu.VMEM((2, tokens.shape[0], TOK_COLS), jnp.bfloat16),
            pltpu.VMEM((2, CAP, hid), jnp.bfloat16),
            pltpu.VMEM((2, CAP, hid), jnp.bfloat16),
            pltpu.VMEM((CAP, hid), jnp.float32),
            pltpu.VMEM((CAP, hid), jnp.float32),
            pltpu.VMEM((CAP, hid), jnp.bfloat16),
            pltpu.VMEM((side, CAP, fd), jnp.float32),
            pltpu.VMEM((side, CAP, fd), jnp.bfloat16),
            pltpu.VMEM((side, CAP, fd), jnp.bfloat16),
            dma((3,)), dma((2,)), dma((n,)), dma((n,)),
            *[dma((2, n // 8, 4)) for _ in range(4)],
            *[dma((2, n // 4, 2)) for _ in range(4)],
            dma((3,)), dma((3,)), dma, dma, dma, dma, dma((2,)), dma((2,)), dma((side,)), dma((side,)),
        ],
        compiler_params=pltpu.CompilerParams(
            collective_id=0, has_side_effects=True, vmem_limit_bytes=60 * 1024 * 1024
        ),
    )(pos, tokens, *(v.reshape(2, half, hid) for v in (gate, up, down)))


def per_device(tokens, expert_ids, keep_mask, route_weight, gate_weight, up_weight, down_weight):
    matches = (expert_ids == 0) & (keep_mask == 1)
    chosen = jnp.any(matches, axis=1).astype(jnp.int32)
    route_sum = jnp.sum(jnp.where(matches, route_weight, jnp.float32(0.0)), axis=1)
    position = jnp.cumsum(chosen) - chosen
    place = jnp.where(chosen == 1, position, -1)
    y = expert(place[None, :], tokens, gate_weight, up_weight, down_weight)
    slot_ids = lax.rem(jnp.arange(2 * CAP, dtype=jnp.int32), CAP)
    combine = (place[:, None] == slot_ids[None, :]).astype(jnp.bfloat16)
    mixed = jnp.dot(combine, y, preferred_element_type=jnp.float32)
    return (mixed * route_sum[:, None]).astype(jnp.bfloat16)


def solution(mesh):
    return jax.shard_map(
        per_device,
        mesh=mesh,
        in_specs=(
            P("wa", None),
            P("wa", None),
            P("wa", None),
            P("wa", None),
            P("wa", "ha"),
            P("wa", "ha"),
            P("wa", "ha"),
        ),
        out_specs=P("wa", "ha"),
        check_vma=False,
    )
```

profile of v0, /device:TPU:3, one launch (start us, length us, event | category | flops | bytes accessed | tf_op | source)
XLA Modules:
  0.0 96.1 jit_solution(10847864239483844496)
XLA Ops:
  0.0 0.8 select_reduce_fusion
  0.9 0.3 reduce-window.9
  1.1 0.1 slice.7
  1.2 0.1 slice_reduce_fusion
  1.4 0.1 fusion.3
  1.4 0.6 compare_select_fusion.pos_ref
  2.0 89.6 %shard_map.73 = bf16[256,2048]{1,0:T(8,128)(2,1)} custom-call(s32[1,1024]{1,0:T(1,128)} %compare_select_fusion.pos_ref, bf16[1024,4096]{1,0:T(8,128)(2,1)} %tok_ref.1, bf16[2,128,768]{2,1,0:T(8,128)(2,1)} %bitcast.10, bf16[2,128,768]{2,1,0:T(8,128)(2,1)} %bitcast.11, bf16[2,128,768]{2,1,0:T(8,128)(2,1)} %bitcast.12), custom_call_target="tpu_custom_call" | custom-call | tf_op jit(solution)/shard_map/pallas_call | solution.py:335
  91.7 4.4 %multiply_convert_fusion = bf16[1024,2048]{1,0:T(8,128)(2,1)} fusion(bf16[256,2048]{1,0:T(8,128)(2,1)} %shard_map.73, f32[1024]{0:T(1024)S(1)} %get-tuple-element.7, s32[256]{0:T(256)S(1)} %iota_and_fusion, s32[1024]{0:T(1024)S(1)} %get-tuple-element.5), kind=kOutput, calls=%fused_computation | convolution fusion | flops 1078198272 | bytes 5252096 | tf_op jit(solution)/shard_map/dot_general | solution.py:376
  (4 shorter events, 0.1 us)
where the time goes:
time: 96.7 us; the launch traced here: 96.1 us
  Pallas kernels  89.6 us (93%)
  matrix products  4.45 us (5%)
  other arithmetic  1.83 us (2%)
    pallas_call x1, Pallas kernels, expert(): pl.pallas_call(functools.partial(expert_kernel, n), out_shape=jax.ShapeDt...  89.6 us
    dot_general x1, matrix products, per_device(): mixed = jnp.dot(combine, y, preferred_element_type=jnp.float32)  4.45 us

commit v1 on v0

v1 whole, which is shorter than its diff:
```python
import functools

import jax
import jax.numpy as jnp
from jax import lax
from jax.experimental import pallas as pl
from jax.experimental.pallas import tpu as pltpu
from jax.sharding import PartitionSpec as P

CAP = 128
MESH = pl.DeviceIdType.MESH


def expert_kernel(
    n,
    pos_ref, route_ref, tok_ref, gate_ref, up_ref, down_ref,
    y_ref,
    w1, w2, stage, tok_buf, guest_out, own_rows, guest_rows, own_acc, guest_acc, part_out, part_in, hidden,
    x_own, x_out, x_in, y_own, y_out, y_in, xy_own, xy_out, xy_in, yx_out, yx_in, count, counts, route,
    load_sem, tok_sem, c_send, c_recv, e_send, e_recv, l1_send, l1_recv, b1_send, b1_recv,
    l2_send, l2_recv, b2_send, b2_recv, g_send, g_recv, p_send, p_recv,
    x_send, x_recv, y_send, y_recv, xy_send, xy_recv, yx_send, yx_recv,
):
    zs = n // 4
    span = zs // 2
    sub = span // 2
    me = lax.axis_index("wa")
    ha = lax.axis_index("ha")
    core = lax.rem(me, 2)
    y = lax.rem(me // 2, 2)
    z = me // 4
    half = z // span
    zl = z - half * span
    sibling = me + 1 - 2 * core
    beside = me + 2 - 4 * y
    mirror = lax.rem(me + n // 2, n)
    q = hidden.shape[2]
    fd = stage.shape[1]
    group = 4 * fd

    def remote(ref, dst, send, recv, **where):
        return pltpu.make_async_remote_copy(
            src_ref=ref, dst_ref=dst, send_sem=send, recv_sem=recv, device_id=where, device_id_type=MESH
        )

    def same(ref, send, recv, **where):
        return remote(ref, ref, send, recv, **where)

    def order(e, at, size):
        short = jnp.minimum(at, size - 1 - at)
        paired = jnp.where(e % 2 == 1, at + (e + 1) // 2, at - e // 2)
        rest = jnp.where(at < size - 1 - at, at + (e - short), at - (e - short))
        return jnp.where(e <= 2 * short, paired, rest)

    class Line:
        def __init__(self, ref_of, at, size, sems):
            self.ref_of, self.at, self.size = ref_of, at, size
            self.l_send, self.l_recv, self.b_send, self.b_recv = sems

        def hop(self, way, *unit):
            to = me + 4 * (1 - 2 * way)
            return same(self.ref_of(core, *unit), self.l_send.at[(way, *unit)], self.l_recv.at[unit], wa=to)

        def up(self, zi):
            return (zi <= self.at) & (self.at + 1 < self.size)

        def down(self, zi):
            return (zi >= self.at) & (self.at > 0)

        def push(self, t, zi, yy):
            @pl.when(self.up(zi))
            def _():
                self.hop(0, t, zi, yy).start()

            @pl.when(self.down(zi))
            def _():
                self.hop(1, t, zi, yy).start()

        def arrive(self, t, zi, yy):
            self.hop(0, t, zi, yy).wait_recv()

        def give(self, t, zi, yy):
            return same(self.ref_of(core, t, zi, yy), self.b_send.at[t, zi, yy], self.b_recv.at[t, zi, yy], wa=sibling)

        def given(self, t, zi, yy):
            return same(
                self.ref_of(1 - core, t, zi, yy), self.b_send.at[t, zi, yy], self.b_recv.at[t, zi, yy], wa=sibling
            )

        def spread(self, t, zi, yy):
            self.push(t, zi, yy)
            self.give(t, zi, yy).start()

        def serve(self, t, zi, yy):
            self.arrive(t, zi, yy)
            self.spread(t, zi, yy)

        def drain(self, kinds):
            @pl.loop(0, self.size)
            def _(zi):
                for t in kinds:
                    for yy in (0, 1):
                        @pl.when(self.up(zi))
                        def _():
                            self.hop(0, t, zi, yy).wait_send()

                        @pl.when(self.down(zi))
                        def _():
                            self.hop(1, t, zi, yy).wait_send()

                        self.give(t, zi, yy).wait_send()

    first = Line(lambda c, t, zi, yy: w1.at[t, zi, yy, c], zl, span, (l1_send, l1_recv, b1_send, b1_recv))
    second = Line(lambda c, t, zi, yy: w2.at[zi, yy, c], z, zs, (l2_send, l2_recv, b2_send, b2_recv))

    def exchange(t):
        dst, recv = (w2.at[z, y, core], l2_recv.at[0, z, y]) if t == 2 else (w1.at[t, zl, y, core], l1_recv.at[t, zl, y])
        return remote(stage.at[t], dst, e_send.at[t], recv, wa=beside)

    def count_copy(k):
        return remote(count, counts.at[me], c_send.at[k], c_recv.at[k], wa=lax.rem(me + k, n))

    def count_got(k):
        return remote(count, counts.at[lax.rem(me - k + n, n)], c_send.at[k], c_recv.at[k], wa=lax.rem(me + k, n))

    def columns(ref, index):
        return ref.at[:, pl.ds(pl.multiple_of(index * q, 128), q)]

    weights = (gate_ref, up_ref, down_ref)
    homes = (w1.at[0, zl, y, core], w1.at[1, zl, y, core], w2.at[z, y, core])
    loads = []
    for t in range(3):
        loads.append((
            pltpu.make_async_copy(columns(weights[t], 1 - y), stage.at[t], load_sem.at[t, 0]),
            pltpu.make_async_copy(columns(weights[t], y), homes[t], load_sem.at[t, 1]),
        ))

    def tok_load(i):
        column = (1 - half) * span + ha * sub + i if i < sub else half * span + i - sub
        return pltpu.make_async_copy(
            tok_ref.at[:, pl.ds(pl.multiple_of(column * group, 128), group)], tok_buf.at[i], tok_sem.at[i]
        )

    for load in loads[0]:
        load.start()
    for i in range(sub):
        tok_load(i).start()
    for load in (*loads[1], *loads[2]):
        load.start()
    for i in range(sub, sub + span):
        tok_load(i).start()

    place = pos_ref[...]
    chosen = jnp.sum(jnp.where(place >= 0, 1, 0), axis=1, keepdims=True)
    count[...] = jnp.broadcast_to(chosen, count.shape)

    barrier = pltpu.get_barrier_semaphore()

    @pl.loop(1, n)
    def _(k):
        pl.semaphore_signal(barrier, inc=1, device_id={"wa": lax.rem(me + k, n)}, device_id_type=MESH)

    pl.semaphore_signal(barrier, inc=1, device_id={"ha": 1 - ha}, device_id_type=MESH)

    slot_ids = lax.broadcasted_iota(jnp.int32, (CAP, pos_ref.shape[1]), 0)
    table = jnp.where(place == slot_ids, jnp.float32(1.0), jnp.float32(0.0)).astype(jnp.bfloat16)
    slot_route = jnp.sum(jnp.where(place == slot_ids, route_ref[...], jnp.float32(0.0)), axis=1, keepdims=True)
    route[...] = jnp.broadcast_to(slot_route, route.shape)

    pl.semaphore_wait(barrier, n)

    def slots(i):
        tok_load(i).wait()
        return jnp.dot(table, tok_buf[i], preferred_element_type=jnp.float32).astype(jnp.bfloat16)

    def direct(ref, yy, sems, k, **where):
        return same(ref.at[pl.ds(ha * sub, sub), yy], sems[0].at[k], sems[1].at[k], **where)

    def other(ref, yy, sems, k, **where):
        return same(ref.at[pl.ds((1 - ha) * sub, sub), yy], sems[0].at[k], sems[1].at[k], **where)

    g_sems = (g_send, g_recv)
    to_x = {"ha": 1 - ha}
    to_y = {"wa": beside}
    guest_send = remote(guest_out, guest_rows.at[pl.ds(ha * sub, sub), y], g_send.at[0], g_recv.at[0], wa=mirror)
    guest_y, guest_y_got = direct(guest_rows, y, g_sems, 1, **to_y), direct(guest_rows, 1 - y, g_sems, 1, **to_y)
    guest_x, guest_x_got = direct(guest_rows, y, g_sems, 2, **to_x), other(guest_rows, y, g_sems, 2, **to_x)
    guest_d, guest_d_got = direct(guest_rows, 1 - y, g_sems, 3, **to_x), other(guest_rows, 1 - y, g_sems, 3, **to_x)
    own_y, own_y_got = direct(own_rows, y, g_sems, 4, **to_y), direct(own_rows, 1 - y, g_sems, 4, **to_y)
    own_d, own_d_got = direct(own_rows, 1 - y, g_sems, 5, **to_x), other(own_rows, 1 - y, g_sems, 5, **to_x)

    for load in loads[0]:
        load.wait()
    exchange(0).start()
    first.spread(0, zl, y)
    for i in range(sub):
        guest_out[i] = slots(i)
    guest_send.start()
    for load in loads[1]:
        load.wait()
    exchange(1).start()
    first.spread(1, zl, y)
    for i in range(span):
        own_rows[i, y] = slots(sub + i)
    own_y.start()
    for load in loads[2]:
        load.wait()
    exchange(2).start()

    @pl.loop(1, n)
    def _(k):
        count_copy(k).start()

    for t in (0, 1):
        first.serve(t, zl, 1 - y)
    second.spread(0, z, y)

    guest_send.wait_recv()
    guest_y.start()
    guest_x.start()
    own_y_got.wait_recv()
    own_d.start()

    def line_in(e):
        zi = order(e, zl, span)
        for yy in (y, 1 - y):
            for t in (0, 1):
                first.serve(t, zi, yy)

    def line_all(e):
        zi = order(e, zl, span)
        for t in (0, 1):
            for yy in (0, 1):
                first.given(t, zi, yy).wait_recv()

    line_all(0)
    second.serve(0, z, 1 - y)
    own_d_got.wait_recv()

    def project(rows, e, t):
        zi = order(e, zl, span)
        return jnp.dot(rows(zi), w1[t, zi].reshape(group, q), preferred_element_type=jnp.float32)

    def guests(yy):
        return lambda zi: guest_rows[zi, yy]

    def mine(zi):
        return own_rows[zi].reshape(2 * CAP, group)

    for t in (0, 1):
        own_acc[t] = project(mine, 0, t)
    guest_y_got.wait_recv()
    guest_d.start()
    guest_x_got.wait_recv()
    for t in (0, 1):
        guest_acc[t] = project(guests(y), 0, t)
    for e in range(1, span):
        line_in(e)
        line_all(e)
        if e + 1 < span:
            for t in (0, 1):
                guest_acc[t] = guest_acc[t] + project(guests(y), e, t)

    def partial(yy):
        return remote(part_out.at[yy], part_in.at[yy], p_send.at[yy], p_recv.at[yy], wa=mirror)

    for t in (0, 1):
        part_out[y, t] = (guest_acc[t] + project(guests(y), span - 1, t)).astype(jnp.bfloat16)
    partial(y).start()
    guest_d_got.wait_recv()
    for t in (0, 1):
        total = project(guests(1 - y), 0, t)
        for e in range(1, span):
            total = total + project(guests(1 - y), e, t)
        part_out[1 - y, t] = total.astype(jnp.bfloat16)
    partial(1 - y).start()

    def line2_in(e):
        zi = order(e, z, zs)
        for yy in (y, 1 - y):
            second.serve(0, zi, yy)

    line2_in(1)
    for t in (0, 1):
        for e in range(1, span):
            own_acc[t] = own_acc[t] + project(mine, e, t)

    @pl.loop(2, span + 1)
    def _(e):
        line2_in(e)

    for yy in (0, 1):
        partial(yy).wait_recv()
    for yy in (0, 1):
        gate = own_acc[0, yy * CAP:(yy + 1) * CAP] + part_in[yy, 0].astype(jnp.float32)
        up = own_acc[1, yy * CAP:(yy + 1) * CAP] + part_in[yy, 1].astype(jnp.float32)
        hidden[yy] = (gate / (1.0 + jnp.exp(-gate)) * up).astype(jnp.bfloat16)

    def swap_x(j):
        return remote(x_out.at[j], x_in.at[j], x_send.at[j], x_recv.at[j], ha=1 - ha)

    def swap_y(zi):
        return remote(y_out.at[zi], y_in.at[zi], y_send.at[zi], y_recv.at[zi], wa=beside)

    def swap_xy(j):
        return remote(xy_out.at[j], xy_in.at[j], xy_send.at[j], xy_recv.at[j], wa=beside)

    def swap_yx(j):
        return remote(yx_out.at[j], yx_in.at[j], yx_send.at[j], yx_recv.at[j], ha=1 - ha)

    def mine_rows(v):
        return jnp.where(y == 0, v[:CAP], v[CAP:]), jnp.where(y == 0, v[CAP:], v[:CAP])

    def down(zi, yy):
        return lax.dot_general(
            hidden[...].reshape(2 * CAP, q), w2[zi, yy].reshape(2 * fd, q), (((1,), (1,)), ((), ())),
            preferred_element_type=jnp.float32,
        )

    def finish(e):
        zi = order(e, z, zs)
        out = zi // span
        j = zi - out * span
        for yy in (0, 1):
            second.given(0, zi, yy).wait_recv()
        part = down(zi, 0)

        @pl.when(out == ha)
        def _():
            x_own[j] = part

        @pl.when(out != ha)
        def _():
            x_out[j] = part.astype(jnp.bfloat16)
            swap_x(j).start()

        keep, leave = mine_rows(down(zi, 1))
        y_out[zi] = leave.astype(jnp.bfloat16)
        swap_y(zi).start()
        y_own[zi] = keep

    def combine(e):
        zi = order(e, z, zs)
        out = zi // span
        j = zi - out * span
        swap_y(zi).wait_recv()
        total = y_own[zi] + y_in[zi].astype(jnp.float32)

        @pl.when(out != ha)
        def _():
            yx_out[j] = total.astype(jnp.bfloat16)
            swap_yx(j).start()

        @pl.when(out == ha)
        def _():
            y_own[zi] = total
            swap_x(j).wait_recv()
            keep, leave = mine_rows(x_own[j] + x_in[j].astype(jnp.float32))
            xy_own[j] = keep
            xy_out[j] = leave.astype(jnp.bfloat16)
            swap_xy(j).start()

    @pl.loop(0, zs)
    def _(e):
        @pl.when(e > span)
        def _():
            line2_in(e)

        finish(e)

        @pl.when(e > 0)
        def _():
            combine(e - 1)

    combine(zs - 1)

    @pl.loop(1, n)
    def _(k):
        count_got(k).wait_recv()

    counts[me] = jnp.zeros(counts.shape[1:], jnp.int32)

    def add_count(i, total):
        return total + jnp.where(i < me, counts[i], 0)

    earlier = lax.fori_loop(0, n, add_count, jnp.zeros(counts.shape[1:], jnp.int32))
    slot = lax.broadcasted_iota(jnp.int32, (CAP, 1), 0)
    scale = jnp.where(slot + earlier[0:1, 0:1] < n // 2 * CAP, route[:, 0:1], jnp.float32(0.0))
    wide = 2 * fd

    for j in range(span):
        swap_xy(j).wait_recv()
        total = xy_own[j] + xy_in[j].astype(jnp.float32)
        y_ref[:, 2 * j * wide:(2 * j + 1) * wide] = (total * scale).astype(jnp.bfloat16)
        swap_yx(j).wait_recv()
        total = y_own[ha * span + j] + yx_in[j].astype(jnp.float32)
        y_ref[:, (2 * j + 1) * wide:(2 * j + 2) * wide] = (total * scale).astype(jnp.bfloat16)

    @pl.loop(1, n)
    def _(k):
        count_copy(k).wait_send()

    for t in range(3):
        exchange(t).wait_send()
    for copy in (guest_send, guest_y, guest_x, guest_d, own_y, own_d, partial(0), partial(1)):
        copy.wait_send()
    first.drain((0, 1))
    second.drain((0,))

    @pl.loop(0, span)
    def _(j):
        swap_x(j).wait_send()
        swap_xy(j).wait_send()
        swap_yx(j).wait_send()

    @pl.loop(0, zs)
    def _(zi):
        swap_y(zi).wait_send()


def expert(pos, route_sum, tokens, gate, up, down):
    n = lax.axis_size("wa")
    fd, hid = gate.shape
    q = hid // 2
    zs = n // 4
    span = zs // 2
    sub = span // 2
    group = 4 * fd
    wide = 2 * fd
    any_spec = pl.BlockSpec(memory_space=pl.ANY)
    vmem = pl.BlockSpec(memory_space=pltpu.VMEM)
    dma = pltpu.SemaphoreType.DMA
    bf16, f32 = jnp.bfloat16, jnp.float32
    return pl.pallas_call(
        functools.partial(expert_kernel, n),
        out_shape=jax.ShapeDtypeStruct((CAP, span * group), bf16),
        in_specs=[vmem, vmem, any_spec, any_spec, any_spec, any_spec],
        out_specs=vmem,
        scratch_shapes=[
            pltpu.VMEM((2, span, 2, 2, fd, q), bf16),
            pltpu.VMEM((zs, 2, 2, fd, q), bf16),
            pltpu.VMEM((3, fd, q), bf16),
            pltpu.VMEM((sub + span, tokens.shape[0], group), bf16),
            pltpu.VMEM((sub, CAP, group), bf16),
            pltpu.VMEM((span, 2, CAP, group), bf16),
            pltpu.VMEM((span, 2, CAP, group), bf16),
            pltpu.VMEM((2, 2 * CAP, q), f32),
            pltpu.VMEM((2, CAP, q), f32),
            pltpu.VMEM((2, 2, CAP, q), bf16),
            pltpu.VMEM((2, 2, CAP, q), bf16),
            pltpu.VMEM((2, CAP, q), bf16),
            pltpu.VMEM((span, 2 * CAP, wide), f32),
            pltpu.VMEM((span, 2 * CAP, wide), bf16),
            pltpu.VMEM((span, 2 * CAP, wide), bf16),
            pltpu.VMEM((zs, CAP, wide), f32),
            pltpu.VMEM((zs, CAP, wide), bf16),
            pltpu.VMEM((zs, CAP, wide), bf16),
            pltpu.VMEM((span, CAP, wide), f32),
            pltpu.VMEM((span, CAP, wide), bf16),
            pltpu.VMEM((span, CAP, wide), bf16),
            pltpu.VMEM((span, CAP, wide), bf16),
            pltpu.VMEM((span, CAP, wide), bf16),
            pltpu.VMEM((8, 128), jnp.int32),
            pltpu.VMEM((n, 8, 128), jnp.int32),
            pltpu.VMEM((CAP, 128), f32),
            dma((3, 2)), dma((sub + span,)), dma((n,)), dma((n,)), dma((3,)), dma((3,)),
            dma((2, 2, span, 2)), dma((2, span, 2)), dma((2, span, 2)), dma((2, span, 2)),
            dma((2, 1, zs, 2)), dma((1, zs, 2)), dma((1, zs, 2)), dma((1, zs, 2)),
            dma((6,)), dma((6,)), dma((2,)), dma((2,)),
            dma((span,)), dma((span,)), dma((zs,)), dma((zs,)),
            dma((span,)), dma((span,)), dma((span,)), dma((span,)),
        ],
        compiler_params=pltpu.CompilerParams(
            collective_id=0, has_side_effects=True, vmem_limit_bytes=60 * 1024 * 1024
        ),
    )(pos, route_sum, tokens, gate, up, down)


def per_device(tokens, expert_ids, keep_mask, route_weight, gate_weight, up_weight, down_weight):
    matches = (expert_ids == 0) & (keep_mask == 1)
    chosen = jnp.any(matches, axis=1).astype(jnp.int32)
    route_sum = jnp.sum(jnp.where(matches, route_weight, jnp.float32(0.0)), axis=1)
    position = jnp.cumsum(chosen) - chosen
    place = jnp.where(chosen == 1, position, -1)
    y = expert(place[None, :], route_sum[None, :], tokens, gate_weight, up_weight, down_weight)
    slot_ids = jnp.arange(CAP, dtype=jnp.int32)
    pick = (place[:, None] == slot_ids[None, :]).astype(jnp.bfloat16)
    return jnp.dot(pick, y, preferred_element_type=jnp.float32).astype(jnp.bfloat16)


def solution(mesh):
    return jax.shard_map(
        per_device,
        mesh=mesh,
        in_specs=(
            P("wa", None),
            P("wa", None),
            P("wa", None),
            P("wa", None),
            P("wa", "ha"),
            P("wa", "ha"),
            P("wa", "ha"),
        ),
        out_specs=P("wa", "ha"),
        check_vma=False,
    )
```

time: 96.7 us -> 94.1 us (0.973)
  Pallas kernels: 89.6 us -> 86.9 us
    pallas_call x1, Pallas kernels: 89.6 us -> 86.9 us  [expert(): pl.pallas_call(functools.partial(expert_kernel, n), out_shape=jax.ShapeDt...]
where the time goes in v1:
time: 94.1 us; the launch traced here: 93.8 us
  Pallas kernels  86.9 us (92%)
  matrix products  4.35 us (5%)
  other arithmetic  2.41 us (3%)
    pallas_call x1, Pallas kernels, expert(): pl.pallas_call(functools.partial(expert_kernel, n), out_shape=jax.ShapeDt...  86.9 us
    dot_general x1, matrix products, per_device(): jnp.dot(pick, y, preferred_element_type=jnp.float32).astype(jnp.bfloat16)  4.35 us

profile of v1, /device:TPU:3, one launch (start us, length us, event | category | flops | bytes accessed | tf_op | source)
XLA Modules:
  0.0 93.8 jit_solution(17746598132765740335)
XLA Ops:
  0.0 1.4 %select_reduce_fusion = (f32[1024]{0:T(1024)}, pred[1024,8]{0,1:T(8,128)(4,1)S(1)}) fusion(f32[1024,8]{0,1:T(8,128)} %param.10, s32[1024,8]{0,1:T(8,128)} %param.9, s32[1024,8]{0,1:T(8,128)} %param.8), kind=kLoop, calls=%fused_computation.3 | loop fusion | flops 39936 | bytes 110592 | tf_op jit(solution)/shard_map/reduce_sum | solution.py:482
  1.4 0.3 reduce-window.9
  1.7 0.1 slice.7
  1.8 0.1 slice_reduce_fusion
  1.9 0.1 fusion.1
  2.0 0.6 compare_select_fusion.pos_ref
  2.6 86.9 %shard_map.73 = bf16[128,2048]{1,0:T(8,128)(2,1)} custom-call(s32[1,1024]{1,0:T(1,128)} %compare_select_fusion.pos_ref, f32[1,1024]{1,0:T(1,128)} %bitcast.8, bf16[1024,4096]{1,0:T(8,128)(2,1)} %tok_ref.1, bf16[256,768]{1,0:T(8,128)(2,1)} %gate_ref.1, bf16[256,768]{1,0:T(8,128)(2,1)} %up_ref.1, bf16[256,768]{1,0:T(8,128)(2,1)} %down_ref.1), custom_call_target="tpu_custom_call" | custom-call | tf_op jit(solution)/shard_map/pallas_call | solution.py:434
  89.5 4.3 %convolution_convert_fusion = bf16[1024,2048]{1,0:T(8,128)(2,1)} fusion(bf16[128,2048]{1,0:T(8,128)(2,1)} %shard_map.73, s32[1024]{0:T(1024)S(1)} %get-tuple-element.5), kind=kOutput, calls=%fused_computation | convolution fusion | flops 539099136 | bytes 4722688 | tf_op jit(solution)/shard_map/dot_general | solution.py:488
  (3 shorter events, 0.1 us)

commit v2 on v1

--- a/solution.py
+++ b/solution.py
@@ -47,10 +47,11 @@
         return remote(ref, ref, send, recv, **where)
 
     def order(e, at, size):
-        short = jnp.minimum(at, size - 1 - at)
+        low = jnp.where(at < size // 2, 1, 0)
+        at = low * at + (1 - low) * (size - 1 - at)
         paired = jnp.where(e % 2 == 1, at + (e + 1) // 2, at - e // 2)
-        rest = jnp.where(at < size - 1 - at, at + (e - short), at - (e - short))
-        return jnp.where(e <= 2 * short, paired, rest)
+        nth = jnp.where(e <= 2 * at, paired, e)
+        return low * nth + (1 - low) * (size - 1 - nth)
 
     class Line:
         def __init__(self, ref_of, at, size, sems):
@@ -188,6 +189,36 @@
     guest_d, guest_d_got = direct(guest_rows, 1 - y, g_sems, 3, **to_x), other(guest_rows, 1 - y, g_sems, 3, **to_x)
     own_y, own_y_got = direct(own_rows, y, g_sems, 4, **to_y), direct(own_rows, 1 - y, g_sems, 4, **to_y)
     own_d, own_d_got = direct(own_rows, 1 - y, g_sems, 5, **to_x), other(own_rows, 1 - y, g_sems, 5, **to_x)
+
+    def line_in(e):
+        zi = order(e, zl, span)
+        for yy in (y, 1 - y):
+            for t in (0, 1):
+                first.serve(t, zi, yy)
+
+    def line_all(e):
+        zi = order(e, zl, span)
+        for t in (0, 1):
+            for yy in (0, 1):
+                first.given(t, zi, yy).wait_recv()
+
+    def line2_in(e):
+        zi = order(e, z, zs)
+        for yy in (0, 1):
+            second.serve(0, zi, yy)
+
+    def project(rows, e, t):
+        zi = order(e, zl, span)
+        return jnp.dot(rows(zi), w1[t, zi].reshape(group, q), preferred_element_type=jnp.float32)
+
+    def guests(yy):
+        return lambda zi: guest_rows[zi, yy]
+
+    def mine(zi):
+        return own_rows[zi].reshape(2 * CAP, group)
+
+    def partial(yy):
+        return remote(part_out.at[yy], part_in.at[yy], p_send.at[yy], p_recv.at[yy], wa=mirror)
 
     for load in loads[0]:
         load.wait()
@@ -200,12 +231,11 @@
         load.wait()
     exchange(1).start()
     first.spread(1, zl, y)
-    for i in range(span):
-        own_rows[i, y] = slots(sub + i)
-    own_y.start()
     for load in loads[2]:
         load.wait()
     exchange(2).start()
+    for i in range(span):
+        own_rows[i, y] = slots(sub + i)
 
     @pl.loop(1, n)
     def _(k):
@@ -214,41 +244,12 @@
     for t in (0, 1):
         first.serve(t, zl, 1 - y)
     second.spread(0, z, y)
-
     guest_send.wait_recv()
     guest_y.start()
     guest_x.start()
-    own_y_got.wait_recv()
-    own_d.start()
-
-    def line_in(e):
-        zi = order(e, zl, span)
-        for yy in (y, 1 - y):
-            for t in (0, 1):
-                first.serve(t, zi, yy)
-
-    def line_all(e):
-        zi = order(e, zl, span)
-        for t in (0, 1):
-            for yy in (0, 1):
-                first.given(t, zi, yy).wait_recv()
-
+    own_y.start()
+    second.serve(0, z, 1 - y)
     line_all(0)
-    second.serve(0, z, 1 - y)
-    own_d_got.wait_recv()
-
-    def project(rows, e, t):
-        zi = order(e, zl, span)
-        return jnp.dot(rows(zi), w1[t, zi].reshape(group, q), preferred_element_type=jnp.float32)
-
-    def guests(yy):
-        return lambda zi: guest_rows[zi, yy]
-
-    def mine(zi):
-        return own_rows[zi].reshape(2 * CAP, group)
-
-    for t in (0, 1):
-        own_acc[t] = project(mine, 0, t)
     guest_y_got.wait_recv()
     guest_d.start()
     guest_x_got.wait_recv()
@@ -260,13 +261,17 @@
         if e + 1 < span:
             for t in (0, 1):
                 guest_acc[t] = guest_acc[t] + project(guests(y), e, t)
-
-    def partial(yy):
-        return remote(part_out.at[yy], part_in.at[yy], p_send.at[yy], p_recv.at[yy], wa=mirror)
-
     for t in (0, 1):
         part_out[y, t] = (guest_acc[t] + project(guests(y), span - 1, t)).astype(jnp.bfloat16)
     partial(y).start()
+    middle = (z > 0) & (z + 1 < zs)
+
+    @pl.when(middle)
+    def _():
+        line2_in(1)
+
+    own_y_got.wait_recv()
+    own_d.start()
     guest_d_got.wait_recv()
     for t in (0, 1):
         total = project(guests(1 - y), 0, t)
@@ -275,20 +280,22 @@
         part_out[1 - y, t] = total.astype(jnp.bfloat16)
     partial(1 - y).start()
 
-    def line2_in(e):
-        zi = order(e, z, zs)
-        for yy in (y, 1 - y):
-            second.serve(0, zi, yy)
-
-    line2_in(1)
+    @pl.when(jnp.logical_not(middle))
+    def _():
+        line2_in(1)
+
+    @pl.when(middle)
+    def _():
+        @pl.loop(2, span + 1)
+        def _(e):
+            line2_in(e)
+
+    own_d_got.wait_recv()
     for t in (0, 1):
+        total = project(mine, 0, t)
         for e in range(1, span):
-            own_acc[t] = own_acc[t] + project(mine, e, t)
-
-    @pl.loop(2, span + 1)
-    def _(e):
-        line2_in(e)
-
+            total = total + project(mine, e, t)
+        own_acc[t] = total
     for yy in (0, 1):
         partial(yy).wait_recv()
     for yy in (0, 1):
@@ -317,27 +324,26 @@
             preferred_element_type=jnp.float32,
         )
 
-    def finish(e):
+    def finish(e, yy):
         zi = order(e, z, zs)
         out = zi // span
         j = zi - out * span
-        for yy in (0, 1):
-            second.given(0, zi, yy).wait_recv()
-        part = down(zi, 0)
-
-        @pl.when(out == ha)
-        def _():
-            x_own[j] = part
-
-        @pl.when(out != ha)
-        def _():
-            x_out[j] = part.astype(jnp.bfloat16)
-            swap_x(j).start()
-
-        keep, leave = mine_rows(down(zi, 1))
-        y_out[zi] = leave.astype(jnp.bfloat16)
-        swap_y(zi).start()
-        y_own[zi] = keep
+        second.given(0, zi, yy).wait_recv()
+        part = down(zi, yy)
+        if yy == 0:
+            @pl.when(out == ha)
+            def _():
+                x_own[j] = part
+
+            @pl.when(out != ha)
+            def _():
+                x_out[j] = part.astype(jnp.bfloat16)
+                swap_x(j).start()
+        else:
+            keep, leave = mine_rows(part)
+            y_out[zi] = leave.astype(jnp.bfloat16)
+            swap_y(zi).start()
+            y_own[zi] = keep
 
     def combine(e):
         zi = order(e, z, zs)
@@ -360,19 +366,49 @@
             xy_out[j] = leave.astype(jnp.bfloat16)
             swap_xy(j).start()
 
-    @pl.loop(0, zs)
+    def late(e):
+        zi = order(e, z, zs)
+        for yy in (0, 1):
+            second.serve(0, zi, yy)
+            finish(e, yy)
+
+    @pl.loop(0, 2)
     def _(e):
-        @pl.when(e > span)
+        finish(e, 0)
+        finish(e, 1)
+
+    @pl.loop(2, span + 1)
+    def _(e):
+        @pl.when(jnp.logical_not(middle))
         def _():
             line2_in(e)
 
-        finish(e)
-
-        @pl.when(e > 0)
-        def _():
-            combine(e - 1)
-
-    combine(zs - 1)
+        finish(e, 0)
+        finish(e, 1)
+
+
+    @pl.when(middle)
+    def _():
+        @pl.loop(span + 1, zs)
+        def _(e):
+            late(e)
+
+
+    @pl.loop(0, span + 1)
+    def _(e):
+        combine(e)
+
+
+    @pl.when(jnp.logical_not(middle))
+    def _():
+        @pl.loop(span + 1, zs)
+        def _(e):
+            late(e)
+
+
+    @pl.loop(span + 1, zs)
+    def _(e):
+        combine(e)
 
     @pl.loop(1, n)
     def _(k):

time: 94.1 us -> 89.6 us (0.952)
  Pallas kernels: 86.9 us -> 82.3 us
    pallas_call x1, Pallas kernels: 86.9 us -> 82.3 us  [expert(): pl.pallas_call(functools.partial(expert_kernel, n), out_shape=jax.ShapeDt...]
where the time goes in v2:
time: 89.6 us; the launch traced here: 89.3 us
  Pallas kernels  82.3 us (92%)
  matrix products  4.35 us (5%)
  other arithmetic  2.41 us (3%)
    pallas_call x1, Pallas kernels, expert(): pl.pallas_call(functools.partial(expert_kernel, n), out_shape=jax.ShapeDt...  82.3 us
    dot_general x1, matrix products, per_device(): jnp.dot(pick, y, preferred_element_type=jnp.float32).astype(jnp.bfloat16)  4.35 us

profile of v2, /device:TPU:3, one launch (start us, length us, event | category | flops | bytes accessed | tf_op | source)
XLA Modules:
  0.0 89.3 jit_solution(11573599571749332255)
XLA Ops:
  0.0 1.4 %select_reduce_fusion = (f32[1024]{0:T(1024)}, pred[1024,8]{0,1:T(8,128)(4,1)S(1)}) fusion(f32[1024,8]{0,1:T(8,128)} %param.10, s32[1024,8]{0,1:T(8,128)} %param.9, s32[1024,8]{0,1:T(8,128)} %param.8), kind=kLoop, calls=%fused_computation.3 | loop fusion | flops 39936 | bytes 110592 | tf_op jit(solution)/shard_map/reduce_sum | solution.py:518
  1.4 0.3 reduce-window.9
  1.7 0.1 slice.7
  1.8 0.1 slice_reduce_fusion
  1.9 0.1 fusion.1
  2.0 0.6 compare_select_fusion.pos_ref
  2.6 82.3 %shard_map.73 = bf16[128,2048]{1,0:T(8,128)(2,1)} custom-call(s32[1,1024]{1,0:T(1,128)} %compare_select_fusion.pos_ref, f32[1,1024]{1,0:T(1,128)} %bitcast.8, bf16[1024,4096]{1,0:T(8,128)(2,1)} %tok_ref.1, bf16[256,768]{1,0:T(8,128)(2,1)} %gate_ref.1, bf16[256,768]{1,0:T(8,128)(2,1)} %up_ref.1, bf16[256,768]{1,0:T(8,128)(2,1)} %down_ref.1), custom_call_target="tpu_custom_call" | custom-call | tf_op jit(solution)/shard_map/pallas_call | solution.py:470
  85.0 4.3 %convolution_convert_fusion = bf16[1024,2048]{1,0:T(8,128)(2,1)} fusion(bf16[128,2048]{1,0:T(8,128)(2,1)} %shard_map.73, s32[1024]{0:T(1024)S(1)} %get-tuple-element.5), kind=kOutput, calls=%fused_computation | convolution fusion | flops 539099136 | bytes 4722688 | tf_op jit(solution)/shard_map/dot_general | solution.py:524
  (3 shorter events, 0.1 us)

commit v3 on v2

--- a/solution.py
+++ b/solution.py
@@ -13,13 +13,13 @@
 
 def expert_kernel(
     n,
-    pos_ref, route_ref, tok_ref, gate_ref, up_ref, down_ref,
-    y_ref,
-    w1, w2, stage, tok_buf, guest_out, own_rows, guest_rows, own_acc, guest_acc, part_out, part_in, hidden,
-    x_own, x_out, x_in, y_own, y_out, y_in, xy_own, xy_out, xy_in, yx_out, yx_in, count, counts, route,
+    ids_ref, keep_ref, route_ref, tok_ref, gate_ref, up_ref, down_ref,
+    y_ref, place_ref,
+    ids, keep, weight, w1, w2, stage, tok_buf, guest_out, own_rows, guest_rows, own_acc, guest_acc, part_out, part_in, hidden,
+    x_own, x_out, x_in, y_own, y_out, y_in, xy_own, xy_out, xy_in, yx_out, yx_in, y_buf, count, counts, route,
     load_sem, tok_sem, c_send, c_recv, e_send, e_recv, l1_send, l1_recv, b1_send, b1_recv,
     l2_send, l2_recv, b2_send, b2_recv, g_send, g_recv, p_send, p_recv,
-    x_send, x_recv, y_send, y_recv, xy_send, xy_recv, yx_send, yx_recv,
+    x_send, x_recv, y_send, y_recv, xy_send, xy_recv, yx_send, yx_recv, out_sem, route_sem,
 ):
     zs = n // 4
     span = zs // 2
@@ -37,6 +37,7 @@
     q = hidden.shape[2]
     fd = stage.shape[1]
     group = 4 * fd
+    wide = 2 * fd
 
     def remote(ref, dst, send, recv, **where):
         return pltpu.make_async_remote_copy(
@@ -52,6 +53,13 @@
         paired = jnp.where(e % 2 == 1, at + (e + 1) // 2, at - e // 2)
         nth = jnp.where(e <= 2 * at, paired, e)
         return low * nth + (1 - low) * (size - 1 - nth)
+
+    def is_late(zi, at, size):
+        low = jnp.where(at < size // 2, 1, 0)
+        at = low * at + (1 - low) * (size - 1 - at)
+        zi = low * zi + (1 - low) * (size - 1 - zi)
+        rank = jnp.where(zi > 2 * at, zi, jnp.where(zi > at, 2 * (zi - at) - 1, 2 * (at - zi)))
+        return (rank > size // 2) | ((at == 0) & ((rank == 1) | (rank > 2)))
 
     class Line:
         def __init__(self, ref_of, at, size, sems):
@@ -142,8 +150,12 @@
             tok_ref.at[:, pl.ds(pl.multiple_of(column * group, 128), group)], tok_buf.at[i], tok_sem.at[i]
         )
 
-    for load in loads[0]:
-        load.start()
+    routing = [
+        pltpu.make_async_copy(ref, buf, route_sem.at[k])
+        for k, (ref, buf) in enumerate(((ids_ref, ids), (keep_ref, keep), (route_ref, weight)))
+    ]
+    for copy in (*loads[0], *routing):
+        copy.start()
     for i in range(sub):
         tok_load(i).start()
     for load in (*loads[1], *loads[2]):
@@ -151,10 +163,6 @@
     for i in range(sub, sub + span):
         tok_load(i).start()
 
-    place = pos_ref[...]
-    chosen = jnp.sum(jnp.where(place >= 0, 1, 0), axis=1, keepdims=True)
-    count[...] = jnp.broadcast_to(chosen, count.shape)
-
     barrier = pltpu.get_barrier_semaphore()
 
     @pl.loop(1, n)
@@ -163,16 +171,7 @@
 
     pl.semaphore_signal(barrier, inc=1, device_id={"ha": 1 - ha}, device_id_type=MESH)
 
-    slot_ids = lax.broadcasted_iota(jnp.int32, (CAP, pos_ref.shape[1]), 0)
-    table = jnp.where(place == slot_ids, jnp.float32(1.0), jnp.float32(0.0)).astype(jnp.bfloat16)
-    slot_route = jnp.sum(jnp.where(place == slot_ids, route_ref[...], jnp.float32(0.0)), axis=1, keepdims=True)
-    route[...] = jnp.broadcast_to(slot_route, route.shape)
-
     pl.semaphore_wait(barrier, n)
-
-    def slots(i):
-        tok_load(i).wait()
-        return jnp.dot(table, tok_buf[i], preferred_element_type=jnp.float32).astype(jnp.bfloat16)
 
     def direct(ref, yy, sems, k, **where):
         return same(ref.at[pl.ds(ha * sub, sub), yy], sems[0].at[k], sems[1].at[k], **where)
@@ -224,8 +223,27 @@
         load.wait()
     exchange(0).start()
     first.spread(0, zl, y)
+    for copy in routing:
+        copy.wait()
+    matches = (ids[...] == 0) & (keep[...] == 1)
+    chosen = jnp.minimum(jnp.sum(jnp.where(matches, 1, 0), axis=0, keepdims=True), 1)
+    route_sum = jnp.sum(jnp.where(matches, weight[...], jnp.float32(0.0)), axis=0, keepdims=True)
+    length = chosen.shape[1]
+    lane = lax.broadcasted_iota(jnp.int32, (8, length), 1)
+    running = jnp.broadcast_to(chosen, (8, length))
+    shift = 1
+    while shift < length:
+        running = running + jnp.where(lane >= shift, pltpu.roll(running, shift, 1), 0)
+        shift *= 2
+    place = jnp.where(chosen == 1, running[0:1] - 1, -1)
+    place_ref[...] = place
+    count[...] = jnp.broadcast_to(jnp.sum(chosen, axis=1, keepdims=True), count.shape)
+    slot_ids = lax.broadcasted_iota(jnp.int32, (CAP, length), 0)
+    hit = place == slot_ids
+    table = jnp.where(hit, jnp.float32(1.0), jnp.float32(0.0)).astype(jnp.bfloat16)
     for i in range(sub):
-        guest_out[i] = slots(i)
+        tok_load(i).wait()
+        guest_out[i] = jnp.dot(table, tok_buf[i], preferred_element_type=jnp.float32).astype(jnp.bfloat16)
     guest_send.start()
     for load in loads[1]:
         load.wait()
@@ -234,8 +252,13 @@
     for load in loads[2]:
         load.wait()
     exchange(2).start()
+    slot_route = jnp.sum(jnp.where(hit, route_sum, jnp.float32(0.0)), axis=1, keepdims=True)
+    route[...] = jnp.broadcast_to(slot_route, route.shape)
     for i in range(span):
-        own_rows[i, y] = slots(sub + i)
+        tok_load(sub + i).wait()
+        own_rows[i, y] = jnp.dot(
+            table, tok_buf[sub + i], preferred_element_type=jnp.float32
+        ).astype(jnp.bfloat16)
 
     @pl.loop(1, n)
     def _(k):
@@ -306,14 +329,14 @@
     def swap_x(j):
         return remote(x_out.at[j], x_in.at[j], x_send.at[j], x_recv.at[j], ha=1 - ha)
 
-    def swap_y(zi):
-        return remote(y_out.at[zi], y_in.at[zi], y_send.at[zi], y_recv.at[zi], wa=beside)
+    def swap_y(zi, yy):
+        return remote(y_out.at[yy, zi], y_in.at[yy, zi], y_send.at[yy, zi], y_recv.at[yy, zi], wa=beside)
 
     def swap_xy(j):
         return remote(xy_out.at[j], xy_in.at[j], xy_send.at[j], xy_recv.at[j], wa=beside)
 
-    def swap_yx(j):
-        return remote(yx_out.at[j], yx_in.at[j], yx_send.at[j], yx_recv.at[j], ha=1 - ha)
+    def swap_yx(j, yy):
+        return remote(yx_out.at[yy, j], yx_in.at[yy, j], yx_send.at[yy, j], yx_recv.at[yy, j], ha=1 - ha)
 
     def mine_rows(v):
         return jnp.where(y == 0, v[:CAP], v[CAP:]), jnp.where(y == 0, v[CAP:], v[:CAP])
@@ -324,91 +347,111 @@
             preferred_element_type=jnp.float32,
         )
 
-    def finish(e, yy):
+    def place_of(e):
         zi = order(e, z, zs)
         out = zi // span
-        j = zi - out * span
+        return zi, out, zi - out * span
+
+    def finish_x(e):
+        zi, out, j = place_of(e)
+        second.given(0, zi, 0).wait_recv()
+        part = down(zi, 0)
+
+        @pl.when(out == ha)
+        def _():
+            x_own[j] = part
+
+        @pl.when(out != ha)
+        def _():
+            x_out[j] = part.astype(jnp.bfloat16)
+            swap_x(j).start()
+
+    def finish_y(e, yy):
+        zi, out, j = place_of(e)
         second.given(0, zi, yy).wait_recv()
-        part = down(zi, yy)
-        if yy == 0:
-            @pl.when(out == ha)
-            def _():
-                x_own[j] = part
-
-            @pl.when(out != ha)
-            def _():
-                x_out[j] = part.astype(jnp.bfloat16)
-                swap_x(j).start()
-        else:
-            keep, leave = mine_rows(part)
-            y_out[zi] = leave.astype(jnp.bfloat16)
-            swap_y(zi).start()
-            y_own[zi] = keep
-
-    def combine(e):
-        zi = order(e, z, zs)
-        out = zi // span
-        j = zi - out * span
-        swap_y(zi).wait_recv()
-        total = y_own[zi] + y_in[zi].astype(jnp.float32)
-
-        @pl.when(out != ha)
-        def _():
-            yx_out[j] = total.astype(jnp.bfloat16)
-            swap_yx(j).start()
+        keep, leave = mine_rows(down(zi, yy))
+        y_out[yy, zi] = leave.astype(jnp.bfloat16)
+        swap_y(zi, yy).start()
+        y_own[yy, zi] = keep
+
+    def combine_x(e):
+        zi, out, j = place_of(e)
 
         @pl.when(out == ha)
         def _():
-            y_own[zi] = total
             swap_x(j).wait_recv()
             keep, leave = mine_rows(x_own[j] + x_in[j].astype(jnp.float32))
             xy_own[j] = keep
             xy_out[j] = leave.astype(jnp.bfloat16)
             swap_xy(j).start()
 
-    def late(e):
-        zi = order(e, z, zs)
-        for yy in (0, 1):
-            second.serve(0, zi, yy)
-            finish(e, yy)
-
-    @pl.loop(0, 2)
-    def _(e):
-        finish(e, 0)
-        finish(e, 1)
-
-    @pl.loop(2, span + 1)
-    def _(e):
-        @pl.when(jnp.logical_not(middle))
-        def _():
-            line2_in(e)
-
-        finish(e, 0)
-        finish(e, 1)
-
+    def combine_y(e, yy):
+        zi, out, j = place_of(e)
+        swap_y(zi, yy).wait_recv()
+        total = y_own[yy, zi] + y_in[yy, zi].astype(jnp.float32)
+
+        @pl.when(out != ha)
+        def _():
+            yx_out[yy, j] = total.astype(jnp.bfloat16)
+            swap_yx(j, yy).start()
+
+        @pl.when(out == ha)
+        def _():
+            y_own[yy, zi] = total
+
+    def late(e, yy):
+        second.serve(0, order(e, z, zs), yy)
+        finish_y(e, yy)
 
     @pl.when(middle)
     def _():
+        @pl.loop(0, span + 1)
+        def _(e):
+            finish_x(e)
+            finish_y(e, 1)
+
         @pl.loop(span + 1, zs)
         def _(e):
-            late(e)
-
-
-    @pl.loop(0, span + 1)
-    def _(e):
-        combine(e)
-
+            late(e, 0)
+            late(e, 1)
+
+        @pl.loop(0, span + 1)
+        def _(e):
+            combine_y(e, 1)
+            combine_x(e)
+
+        @pl.loop(span + 1, zs)
+        def _(e):
+            combine_y(e, 0)
+            combine_y(e, 1)
 
     @pl.when(jnp.logical_not(middle))
     def _():
-        @pl.loop(span + 1, zs)
+        finish_y(0, 1)
+        finish_x(0)
+        finish_y(1, 0)
+        finish_y(1, 1)
+        second.serve(0, order(2, z, zs), 0)
+        finish_x(2)
+        late(2, 1)
+        combine_y(0, 1)
+        combine_x(0)
+        combine_y(1, 0)
+        combine_y(1, 1)
+
+        @pl.loop(3, zs - 1)
         def _(e):
-            late(e)
-
-
-    @pl.loop(span + 1, zs)
-    def _(e):
-        combine(e)
+            late(e, 0)
+            late(e, 1)
+            combine_y(e, 0)
+            combine_y(e, 1)
+
+        late(zs - 1, 0)
+        combine_y(2, 1)
+        combine_x(2)
+        late(zs - 1, 1)
+        combine_y(zs - 1, 0)
+        combine_y(zs - 1, 1)
 
     @pl.loop(1, n)
     def _(k):
@@ -422,15 +465,36 @@
     earlier = lax.fori_loop(0, n, add_count, jnp.zeros(counts.shape[1:], jnp.int32))
     slot = lax.broadcasted_iota(jnp.int32, (CAP, 1), 0)
     scale = jnp.where(slot + earlier[0:1, 0:1] < n // 2 * CAP, route[:, 0:1], jnp.float32(0.0))
-    wide = 2 * fd
-
-    for j in range(span):
-        swap_xy(j).wait_recv()
-        total = xy_own[j] + xy_in[j].astype(jnp.float32)
-        y_ref[:, 2 * j * wide:(2 * j + 1) * wide] = (total * scale).astype(jnp.bfloat16)
-        swap_yx(j).wait_recv()
-        total = y_own[ha * span + j] + yx_in[j].astype(jnp.float32)
-        y_ref[:, (2 * j + 1) * wide:(2 * j + 2) * wide] = (total * scale).astype(jnp.bfloat16)
+    width = 2 * span * wide
+    cut = wide if wide % 128 == 0 else width
+
+    def out_copy(u):
+        return pltpu.make_async_copy(y_buf.at[:, u * cut:(u + 1) * cut], y_ref.at[:, u * cut:(u + 1) * cut], out_sem.at[u])
+
+    for yy in (1, 0):
+        for j in range(span):
+            zi = ha * span + j
+            u = 2 * j + yy
+            if yy == 0:
+                behind = is_late(zi, z, zs)
+
+                @pl.when(behind)
+                def _():
+                    swap_yx(j, 0).wait_recv()
+                    y_buf[:, u * wide:(u + 1) * wide] = ((y_own[0, zi] + yx_in[0, j].astype(jnp.float32)) * scale).astype(jnp.bfloat16)
+
+                @pl.when(jnp.logical_not(behind))
+                def _():
+                    swap_xy(j).wait_recv()
+                    y_buf[:, u * wide:(u + 1) * wide] = ((xy_own[j] + xy_in[j].astype(jnp.float32)) * scale).astype(jnp.bfloat16)
+            else:
+                swap_yx(j, 1).wait_recv()
+                y_buf[:, u * wide:(u + 1) * wide] = ((y_own[1, zi] + yx_in[1, j].astype(jnp.float32)) * scale).astype(jnp.bfloat16)
+            if cut == wide:
+                out_copy(u).start()
+
+    if cut != wide:
+        out_copy(0).start()
 
     @pl.loop(1, n)
     def _(k):
@@ -443,18 +507,40 @@
     first.drain((0, 1))
     second.drain((0,))
 
-    @pl.loop(0, span)
-    def _(j):
-        swap_x(j).wait_send()
-        swap_xy(j).wait_send()
-        swap_yx(j).wait_send()
-
     @pl.loop(0, zs)
-    def _(zi):
-        swap_y(zi).wait_send()
-
-
-def expert(pos, route_sum, tokens, gate, up, down):
+    def _(e):
+        zi, out, j = place_of(e)
+        swap_y(zi, 1).wait_send()
+
+        @pl.when(out != ha)
+        def _():
+            swap_yx(j, 1).wait_send()
+
+        behind = is_late(zi, z, zs)
+
+        @pl.when(behind)
+        def _():
+            swap_y(zi, 0).wait_send()
+
+            @pl.when(out != ha)
+            def _():
+                swap_yx(j, 0).wait_send()
+
+        @pl.when(jnp.logical_not(behind))
+        def _():
+            @pl.when(out != ha)
+            def _():
+                swap_x(j).wait_send()
+
+            @pl.when(out == ha)
+            def _():
+                swap_xy(j).wait_send()
+
+    for u in range(width // cut):
+        out_copy(u).wait()
+
+
+def expert(ids, keep, weight, tokens, gate, up, down):
     n = lax.axis_size("wa")
     fd, hid = gate.shape
     q = hid // 2
@@ -469,10 +555,15 @@
     bf16, f32 = jnp.bfloat16, jnp.float32
     return pl.pallas_call(
         functools.partial(expert_kernel, n),
-        out_shape=jax.ShapeDtypeStruct((CAP, span * group), bf16),
-        in_specs=[vmem, vmem, any_spec, any_spec, any_spec, any_spec],
-        out_specs=vmem,
+        out_shape=(
+            jax.ShapeDtypeStruct((CAP, span * group), bf16), jax.ShapeDtypeStruct((1, tokens.shape[0]), jnp.int32)
+        ),
+        in_specs=[any_spec] * 7,
+        out_specs=(any_spec, vmem),
         scratch_shapes=[
+            pltpu.VMEM(ids.shape, jnp.int32),
+            pltpu.VMEM(ids.shape, jnp.int32),
+            pltpu.VMEM(ids.shape, f32),
             pltpu.VMEM((2, span, 2, 2, fd, q), bf16),
             pltpu.VMEM((zs, 2, 2, fd, q), bf16),
             pltpu.VMEM((3, fd, q), bf16),
@@ -488,14 +579,15 @@
             pltpu.VMEM((span, 2 * CAP, wide), f32),
             pltpu.VMEM((span, 2 * CAP, wide), bf16),
             pltpu.VMEM((span, 2 * CAP, wide), bf16),
-            pltpu.VMEM((zs, CAP, wide), f32),
-            pltpu.VMEM((zs, CAP, wide), bf16),
-            pltpu.VMEM((zs, CAP, wide), bf16),
+            pltpu.VMEM((2, zs, CAP, wide), f32),
+            pltpu.VMEM((2, zs, CAP, wide), bf16),
+            pltpu.VMEM((2, zs, CAP, wide), bf16),
             pltpu.VMEM((span, CAP, wide), f32),
             pltpu.VMEM((span, CAP, wide), bf16),
             pltpu.VMEM((span, CAP, wide), bf16),
-            pltpu.VMEM((span, CAP, wide), bf16),
-            pltpu.VMEM((span, CAP, wide), bf16),
+            pltpu.VMEM((2, span, CAP, wide), bf16),
+            pltpu.VMEM((2, span, CAP, wide), bf16),
+            pltpu.VMEM((CAP, 2 * span * wide), bf16),
             pltpu.VMEM((8, 128), jnp.int32),
             pltpu.VMEM((n, 8, 128), jnp.int32),
             pltpu.VMEM((CAP, 128), f32),
@@ -503,22 +595,18 @@
             dma((2, 2, span, 2)), dma((2, span, 2)), dma((2, span, 2)), dma((2, span, 2)),
             dma((2, 1, zs, 2)), dma((1, zs, 2)), dma((1, zs, 2)), dma((1, zs, 2)),
             dma((6,)), dma((6,)), dma((2,)), dma((2,)),
-            dma((span,)), dma((span,)), dma((zs,)), dma((zs,)),
-            dma((span,)), dma((span,)), dma((span,)), dma((span,)),
+            dma((span,)), dma((span,)), dma((2, zs)), dma((2, zs)),
+            dma((span,)), dma((span,)), dma((2, span)), dma((2, span)), dma((2 * span,)), dma((3,)),
         ],
         compiler_params=pltpu.CompilerParams(
             collective_id=0, has_side_effects=True, vmem_limit_bytes=60 * 1024 * 1024
         ),
-    )(pos, route_sum, tokens, gate, up, down)
+    )(ids, keep, weight, tokens, gate, up, down)
 
 
 def per_device(tokens, expert_ids, keep_mask, route_weight, gate_weight, up_weight, down_weight):
-    matches = (expert_ids == 0) & (keep_mask == 1)
-    chosen = jnp.any(matches, axis=1).astype(jnp.int32)
-    route_sum = jnp.sum(jnp.where(matches, route_weight, jnp.float32(0.0)), axis=1)
-    position = jnp.cumsum(chosen) - chosen
-    place = jnp.where(chosen == 1, position, -1)
-    y = expert(place[None, :], route_sum[None, :], tokens, gate_weight, up_weight, down_weight)
+    y, place = expert(expert_ids.T, keep_mask.T, route_weight.T, tokens, gate_weight, up_weight, down_weight)
+    place = place[0]
     slot_ids = jnp.arange(CAP, dtype=jnp.int32)
     pick = (place[:, None] == slot_ids[None, :]).astype(jnp.bfloat16)
     return jnp.dot(pick, y, preferred_element_type=jnp.float32).astype(jnp.bfloat16)

time: 89.6 us -> 84.6 us (0.944)
  other arithmetic: 2.41 us -> 0 us
  Pallas kernels: 82.3 us -> 80.1 us
    pallas_call x1, Pallas kernels: 82.3 us -> 80.1 us  [expert(): pl.pallas_call(functools.partial(expert_kernel, n), out_shape=(jax.ShapeD...]
    reduce_sum x1 -> x0, other arithmetic: 1.4 us -> none  [per_device(): jnp.sum(jnp.where(matches, route_weight, jnp.float32(0.0)), axis=1)]
where the time goes in v3:
time: 84.6 us; the launch traced here: 84.4 us
  Pallas kernels  80.1 us (95%)
  matrix products  4.35 us (5%)
    pallas_call x1, Pallas kernels, expert(): pl.pallas_call(functools.partial(expert_kernel, n), out_shape=(jax.ShapeD...  80.1 us
    dot_general x1, matrix products, per_device(): jnp.dot(pick, y, preferred_element_type=jnp.float32).astype(jnp.bfloat16)  4.35 us

profile of v3, /device:TPU:3, one launch (start us, length us, event | category | flops | bytes accessed | tf_op | source)
XLA Modules:
  0.0 84.4 jit_solution(7233840223875927453)
XLA Ops:
  0.0 80.1 %shard_map.73 = (bf16[128,2048]{1,0:T(8,128)(2,1)}, s32[1,1024]{1,0:T(1,128)}) custom-call(s32[8,1024]{1,0:T(8,128)} %bitcast.5, s32[8,1024]{1,0:T(8,128)} %bitcast.6, f32[8,1024]{1,0:T(8,128)} %bitcast.7, bf16[1024,4096]{1,0:T(8,128)(2,1)} %tok_ref.1, bf16[256,768]{1,0:T(8,128)(2,1)} %gate_ref.1, bf16[256,768]{1,0:T(8,128)(2,1)} %up_ref.1, ...), custom_call_target="tpu_custom_call" | custom-call | tf_op jit(solution)/shard_map/pallas_call | solution.py:556
  80.1 4.4 %convolution_convert_fusion = bf16[1024,2048]{1,0:T(8,128)(2,1)} fusion(bf16[128,2048]{1,0:T(8,128)(2,1)} %get-tuple-element.8, s32[1024]{0:T(1024)} %bitcast.8), kind=kOutput, calls=%fused_computation | convolution fusion | flops 539099136 | bytes 4722688 | tf_op jit(solution)/shard_map/dot_general | solution.py:612

commit v4 on v3

--- a/solution.py
+++ b/solution.py
@@ -15,11 +15,11 @@
     n,
     ids_ref, keep_ref, route_ref, tok_ref, gate_ref, up_ref, down_ref,
     y_ref, place_ref,
-    ids, keep, weight, w1, w2, stage, tok_buf, guest_out, own_rows, guest_rows, own_acc, guest_acc, part_out, part_in, hidden,
+    ids, keep, weight, place_buf, w1, w2, stage, tok_buf, guest_out, own_rows, guest_rows, own_acc, guest_acc, part_out, part_in, hidden,
     x_own, x_out, x_in, y_own, y_out, y_in, xy_own, xy_out, xy_in, yx_out, yx_in, y_buf, count, counts, route,
-    load_sem, tok_sem, c_send, c_recv, e_send, e_recv, l1_send, l1_recv, b1_send, b1_recv,
-    l2_send, l2_recv, b2_send, b2_recv, g_send, g_recv, p_send, p_recv,
-    x_send, x_recv, y_send, y_recv, xy_send, xy_recv, yx_send, yx_recv, out_sem, route_sem,
+    load_sem, tok_sem, c_sem, e_send, l1_send, l1_recv, b1_send, b1_recv, l2_send, l2_recv, b2_send, b2_recv,
+    g_send, g_recv, p_send, p_recv, x_send, x_recv, y_send, y_recv, xy_send, xy_recv, yx_send, yx_recv,
+    part_send, part_recv, out_sem, route_sem,
 ):
     zs = n // 4
     span = zs // 2
@@ -54,12 +54,22 @@
         nth = jnp.where(e <= 2 * at, paired, e)
         return low * nth + (1 - low) * (size - 1 - nth)
 
-    def is_late(zi, at, size):
+    def rank_of(zi, at, size):
         low = jnp.where(at < size // 2, 1, 0)
         at = low * at + (1 - low) * (size - 1 - at)
         zi = low * zi + (1 - low) * (size - 1 - zi)
-        rank = jnp.where(zi > 2 * at, zi, jnp.where(zi > at, 2 * (zi - at) - 1, 2 * (at - zi)))
-        return (rank > size // 2) | ((at == 0) & ((rank == 1) | (rank > 2)))
+        return jnp.where(zi > 2 * at, zi, jnp.where(zi > at, 2 * (zi - at) - 1, 2 * (at - zi)))
+
+    def is_late(zi, at, size):
+        rank = rank_of(zi, at, size)
+        edge = (at == 0) | (at + 1 == size)
+        return (rank > size // 2) | (edge & ((rank == 1) | (rank > 2)))
+
+    def settle(sem, elements):
+        rows = elements // group
+        tokens = tok_buf.shape[1]
+        for size in [tokens] * (rows // tokens) + [rows % tokens] * (rows % tokens > 0):
+            same(tok_buf.at[0, 0:size], sem, sem, wa=sibling).wait_send()
 
     class Line:
         def __init__(self, ref_of, at, size, sems):
@@ -68,7 +78,7 @@
 
         def hop(self, way, *unit):
             to = me + 4 * (1 - 2 * way)
-            return same(self.ref_of(core, *unit), self.l_send.at[(way, *unit)], self.l_recv.at[unit], wa=to)
+            return same(self.ref_of(core, *unit), self.l_send, self.l_recv.at[unit], wa=to)
 
         def up(self, zi):
             return (zi <= self.at) & (self.at + 1 < self.size)
@@ -89,12 +99,10 @@
             self.hop(0, t, zi, yy).wait_recv()
 
         def give(self, t, zi, yy):
-            return same(self.ref_of(core, t, zi, yy), self.b_send.at[t, zi, yy], self.b_recv.at[t, zi, yy], wa=sibling)
+            return same(self.ref_of(core, t, zi, yy), self.b_send, self.b_recv(t, zi, yy), wa=sibling)
 
         def given(self, t, zi, yy):
-            return same(
-                self.ref_of(1 - core, t, zi, yy), self.b_send.at[t, zi, yy], self.b_recv.at[t, zi, yy], wa=sibling
-            )
+            return same(self.ref_of(1 - core, t, zi, yy), self.b_send, self.b_recv(t, zi, yy), wa=sibling)
 
         def spread(self, t, zi, yy):
             self.push(t, zi, yy)
@@ -105,32 +113,31 @@
             self.spread(t, zi, yy)
 
         def drain(self, kinds):
-            @pl.loop(0, self.size)
-            def _(zi):
-                for t in kinds:
-                    for yy in (0, 1):
-                        @pl.when(self.up(zi))
-                        def _():
-                            self.hop(0, t, zi, yy).wait_send()
-
-                        @pl.when(self.down(zi))
-                        def _():
-                            self.hop(1, t, zi, yy).wait_send()
-
-                        self.give(t, zi, yy).wait_send()
-
-    first = Line(lambda c, t, zi, yy: w1.at[t, zi, yy, c], zl, span, (l1_send, l1_recv, b1_send, b1_recv))
-    second = Line(lambda c, t, zi, yy: w2.at[zi, yy, c], z, zs, (l2_send, l2_recv, b2_send, b2_recv))
+            edge = (self.at == 0) | (self.at + 1 == self.size)
+            unit = 2 * kinds * fd * q
+
+            @pl.when(edge)
+            def _():
+                settle(self.l_send, unit)
+
+            @pl.when(jnp.logical_not(edge))
+            def _():
+                settle(self.l_send, (self.size + 1) * unit)
+
+            settle(self.b_send, self.size * unit)
+
+    first = Line(lambda c, t, zi, yy: w1.at[t, zi, yy, c], zl, span, (l1_send, l1_recv, b1_send, lambda t, zi, yy: b1_recv.at[zi]))
+    second = Line(lambda c, t, zi, yy: w2.at[zi, yy, c], z, zs, (l2_send, l2_recv, b2_send, lambda t, zi, yy: b2_recv.at[zi, yy]))
 
     def exchange(t):
         dst, recv = (w2.at[z, y, core], l2_recv.at[0, z, y]) if t == 2 else (w1.at[t, zl, y, core], l1_recv.at[t, zl, y])
-        return remote(stage.at[t], dst, e_send.at[t], recv, wa=beside)
+        return remote(stage.at[t], dst, e_send, recv, wa=beside)
 
     def count_copy(k):
-        return remote(count, counts.at[me], c_send.at[k], c_recv.at[k], wa=lax.rem(me + k, n))
-
-    def count_got(k):
-        return remote(count, counts.at[lax.rem(me - k + n, n)], c_send.at[k], c_recv.at[k], wa=lax.rem(me + k, n))
+        return remote(count, counts.at[me], c_sem.at[0], c_sem.at[1], wa=lax.rem(me + k, n))
+
+    def all_counts():
+        return same(counts.at[pl.ds(0, n - 1)], c_sem.at[0], c_sem.at[1], wa=sibling)
 
     def columns(ref, index):
         return ref.at[:, pl.ds(pl.multiple_of(index * q, 128), q)]
@@ -140,9 +147,12 @@
     loads = []
     for t in range(3):
         loads.append((
-            pltpu.make_async_copy(columns(weights[t], 1 - y), stage.at[t], load_sem.at[t, 0]),
-            pltpu.make_async_copy(columns(weights[t], y), homes[t], load_sem.at[t, 1]),
+            pltpu.make_async_copy(columns(weights[t], 1 - y), stage.at[t], load_sem.at[t]),
+            pltpu.make_async_copy(columns(weights[t], y), homes[t], load_sem.at[t]),
         ))
+
+    def loaded(t):
+        pltpu.make_async_copy(w1.at[0, 0, 0], w1.at[0, 0, 0], load_sem.at[t]).wait()
 
     def tok_load(i):
         column = (1 - half) * span + ha * sub + i if i < sub else half * span + i - sub
@@ -174,15 +184,15 @@
     pl.semaphore_wait(barrier, n)
 
     def direct(ref, yy, sems, k, **where):
-        return same(ref.at[pl.ds(ha * sub, sub), yy], sems[0].at[k], sems[1].at[k], **where)
+        return same(ref.at[pl.ds(ha * sub, sub), yy], sems[0], sems[1].at[k], **where)
 
     def other(ref, yy, sems, k, **where):
-        return same(ref.at[pl.ds((1 - ha) * sub, sub), yy], sems[0].at[k], sems[1].at[k], **where)
+        return same(ref.at[pl.ds((1 - ha) * sub, sub), yy], sems[0], sems[1].at[k], **where)
 
     g_sems = (g_send, g_recv)
     to_x = {"ha": 1 - ha}
     to_y = {"wa": beside}
-    guest_send = remote(guest_out, guest_rows.at[pl.ds(ha * sub, sub), y], g_send.at[0], g_recv.at[0], wa=mirror)
+    guest_send = remote(guest_out, guest_rows.at[pl.ds(ha * sub, sub), y], g_send, g_recv.at[0], wa=mirror)
     guest_y, guest_y_got = direct(guest_rows, y, g_sems, 1, **to_y), direct(guest_rows, 1 - y, g_sems, 1, **to_y)
     guest_x, guest_x_got = direct(guest_rows, y, g_sems, 2, **to_x), other(guest_rows, y, g_sems, 2, **to_x)
     guest_d, guest_d_got = direct(guest_rows, 1 - y, g_sems, 3, **to_x), other(guest_rows, 1 - y, g_sems, 3, **to_x)
@@ -197,9 +207,7 @@
 
     def line_all(e):
         zi = order(e, zl, span)
-        for t in (0, 1):
-            for yy in (0, 1):
-                first.given(t, zi, yy).wait_recv()
+        same(w1.at[:, zi, :, 1 - core], b1_send, b1_recv.at[zi], wa=sibling).wait_recv()
 
     def line2_in(e):
         zi = order(e, z, zs)
@@ -217,10 +225,9 @@
         return own_rows[zi].reshape(2 * CAP, group)
 
     def partial(yy):
-        return remote(part_out.at[yy], part_in.at[yy], p_send.at[yy], p_recv.at[yy], wa=mirror)
-
-    for load in loads[0]:
-        load.wait()
+        return remote(part_out.at[yy], part_in.at[yy], p_send, p_recv.at[yy], wa=mirror)
+
+    loaded(0)
     exchange(0).start()
     first.spread(0, zl, y)
     for copy in routing:
@@ -236,7 +243,9 @@
         running = running + jnp.where(lane >= shift, pltpu.roll(running, shift, 1), 0)
         shift *= 2
     place = jnp.where(chosen == 1, running[0:1] - 1, -1)
-    place_ref[...] = place
+    place_buf[...] = place
+    place_copy = pltpu.make_async_copy(place_buf, place_ref, route_sem.at[3])
+    place_copy.start()
     count[...] = jnp.broadcast_to(jnp.sum(chosen, axis=1, keepdims=True), count.shape)
     slot_ids = lax.broadcasted_iota(jnp.int32, (CAP, length), 0)
     hit = place == slot_ids
@@ -245,12 +254,10 @@
         tok_load(i).wait()
         guest_out[i] = jnp.dot(table, tok_buf[i], preferred_element_type=jnp.float32).astype(jnp.bfloat16)
     guest_send.start()
-    for load in loads[1]:
-        load.wait()
+    loaded(1)
     exchange(1).start()
     first.spread(1, zl, y)
-    for load in loads[2]:
-        load.wait()
+    loaded(2)
     exchange(2).start()
     slot_route = jnp.sum(jnp.where(hit, route_sum, jnp.float32(0.0)), axis=1, keepdims=True)
     route[...] = jnp.broadcast_to(slot_route, route.shape)
@@ -330,7 +337,15 @@
         return remote(x_out.at[j], x_in.at[j], x_send.at[j], x_recv.at[j], ha=1 - ha)
 
     def swap_y(zi, yy):
-        return remote(y_out.at[yy, zi], y_in.at[yy, zi], y_send.at[yy, zi], y_recv.at[yy, zi], wa=beside)
+        return remote(y_out.at[yy, zi], y_in.at[yy, zi], y_send, y_recv.at[yy, zi], wa=beside)
+
+    def swap_part(zi, yy, c):
+        return remote(y_out.at[yy, zi, c], y_in.at[yy, zi, c], y_send, part_recv.at[0, yy, c], wa=beside)
+
+    def swap_part_x(j, yy, c):
+        return remote(
+            yx_out.at[yy, j, c], yx_in.at[yy, j, c], part_send.at[yy, c], part_recv.at[1, yy, c], ha=1 - ha
+        )
 
     def swap_xy(j):
         return remote(xy_out.at[j], xy_in.at[j], xy_send.at[j], xy_recv.at[j], wa=beside)
@@ -370,9 +385,11 @@
         zi, out, j = place_of(e)
         second.given(0, zi, yy).wait_recv()
         keep, leave = mine_rows(down(zi, yy))
-        y_out[yy, zi] = leave.astype(jnp.bfloat16)
+        for c in (0, 1):
+            y_out[yy, zi, c] = leave[:, c * fd:(c + 1) * fd].astype(jnp.bfloat16)
         swap_y(zi, yy).start()
-        y_own[yy, zi] = keep
+        for c in (0, 1):
+            y_own[yy, zi, c] = keep[:, c * fd:(c + 1) * fd]
 
     def combine_x(e):
         zi, out, j = place_of(e)
@@ -398,6 +415,35 @@
         @pl.when(out == ha)
         def _():
             y_own[yy, zi] = total
+
+    def finish_last(yy):
+        zi, out, j = place_of(zs - 1)
+        second.serve(0, zi, yy)
+        for c in (core, 1 - core):
+            if c is not core:
+                second.given(0, zi, yy).wait_recv()
+            keep, leave = mine_rows(lax.dot_general(
+                hidden[...].reshape(2 * CAP, q), w2[zi, yy, c], (((1,), (1,)), ((), ())),
+                preferred_element_type=jnp.float32,
+            ))
+            y_out[yy, zi, c] = leave.astype(jnp.bfloat16)
+            swap_part(zi, yy, c).start()
+            y_own[yy, zi, c] = keep
+
+    def combine_last(yy):
+        zi, out, j = place_of(zs - 1)
+        for c in (core, 1 - core):
+            swap_part(zi, yy, c).wait_recv()
+            total = y_own[yy, zi, c] + y_in[yy, zi, c].astype(jnp.float32)
+
+            @pl.when(out != ha)
+            def _():
+                yx_out[yy, j, c] = total.astype(jnp.bfloat16)
+                swap_part_x(j, yy, c).start()
+
+            @pl.when(out == ha)
+            def _():
+                y_own[yy, zi, c] = total
 
     def late(e, yy):
         second.serve(0, order(e, z, zs), yy)
@@ -410,20 +456,26 @@
             finish_x(e)
             finish_y(e, 1)
 
-        @pl.loop(span + 1, zs)
+        @pl.loop(span + 1, zs - 1)
         def _(e):
             late(e, 0)
             late(e, 1)
+
+        finish_last(0)
+        finish_last(1)
 
         @pl.loop(0, span + 1)
         def _(e):
             combine_y(e, 1)
             combine_x(e)
 
-        @pl.loop(span + 1, zs)
+        @pl.loop(span + 1, zs - 1)
         def _(e):
             combine_y(e, 0)
             combine_y(e, 1)
+
+        combine_last(0)
+        combine_last(1)
 
     @pl.when(jnp.logical_not(middle))
     def _():
@@ -437,7 +489,6 @@
         combine_y(0, 1)
         combine_x(0)
         combine_y(1, 0)
-        combine_y(1, 1)
 
         @pl.loop(3, zs - 1)
         def _(e):
@@ -446,16 +497,15 @@
             combine_y(e, 0)
             combine_y(e, 1)
 
-        late(zs - 1, 0)
+        finish_last(0)
+        combine_y(1, 1)
         combine_y(2, 1)
         combine_x(2)
-        late(zs - 1, 1)
-        combine_y(zs - 1, 0)
-        combine_y(zs - 1, 1)
-
-    @pl.loop(1, n)
-    def _(k):
-        count_got(k).wait_recv()
+        finish_last(1)
+        combine_last(0)
+        combine_last(1)
+
+    all_counts().wait_recv()
 
     counts[me] = jnp.zeros(counts.shape[1:], jnp.int32)
 
@@ -469,75 +519,93 @@
     cut = wide if wide % 128 == 0 else width
 
     def out_copy(u):
-        return pltpu.make_async_copy(y_buf.at[:, u * cut:(u + 1) * cut], y_ref.at[:, u * cut:(u + 1) * cut], out_sem.at[u])
+        return pltpu.make_async_copy(y_buf.at[:, u * cut:(u + 1) * cut], y_ref.at[:, u * cut:(u + 1) * cut], out_sem)
+
+    def put(u, total):
+        y_buf[:, u * wide:(u + 1) * wide] = (total * scale).astype(jnp.bfloat16)
+
+    def put_y(u, zi, yy, j):
+        for c in (0, 1):
+            total = y_own[yy, zi, c] + yx_in[yy, j, c].astype(jnp.float32)
+            y_buf[:, u * wide + c * fd:u * wide + (c + 1) * fd] = (total * scale).astype(jnp.bfloat16)
 
     for yy in (1, 0):
         for j in range(span):
             zi = ha * span + j
             u = 2 * j + yy
+            final = rank_of(zi, z, zs) == zs - 1
+            split = is_late(zi, z, zs) if yy == 0 else final | True
+
+            @pl.when(final)
+            def _():
+                for c in (core, 1 - core):
+                    swap_part_x(j, yy, c).wait_recv()
+
+            @pl.when(split & jnp.logical_not(final))
+            def _():
+                swap_yx(j, yy).wait_recv()
+
+            @pl.when(split)
+            def _():
+                put_y(u, zi, yy, j)
+
             if yy == 0:
-                behind = is_late(zi, z, zs)
-
-                @pl.when(behind)
-                def _():
-                    swap_yx(j, 0).wait_recv()
-                    y_buf[:, u * wide:(u + 1) * wide] = ((y_own[0, zi] + yx_in[0, j].astype(jnp.float32)) * scale).astype(jnp.bfloat16)
-
-                @pl.when(jnp.logical_not(behind))
+                @pl.when(jnp.logical_not(split))
                 def _():
                     swap_xy(j).wait_recv()
-                    y_buf[:, u * wide:(u + 1) * wide] = ((xy_own[j] + xy_in[j].astype(jnp.float32)) * scale).astype(jnp.bfloat16)
-            else:
-                swap_yx(j, 1).wait_recv()
-                y_buf[:, u * wide:(u + 1) * wide] = ((y_own[1, zi] + yx_in[1, j].astype(jnp.float32)) * scale).astype(jnp.bfloat16)
+                    put(u, xy_own[j] + xy_in[j].astype(jnp.float32))
+
             if cut == wide:
                 out_copy(u).start()
 
     if cut != wide:
         out_copy(0).start()
 
-    @pl.loop(1, n)
-    def _(k):
-        count_copy(k).wait_send()
-
-    for t in range(3):
-        exchange(t).wait_send()
-    for copy in (guest_send, guest_y, guest_x, guest_d, own_y, own_d, partial(0), partial(1)):
-        copy.wait_send()
-    first.drain((0, 1))
-    second.drain((0,))
+    all_counts().wait_send()
+
+    place_copy.wait()
+    settle(e_send, 3 * fd * q)
+    settle(g_send, 6 * sub * CAP * group)
+    settle(p_send, 4 * CAP * q)
+    first.drain(2)
+    second.drain(1)
+
+    @pl.when(middle)
+    def _():
+        settle(y_send, (zs + zs - 1 - span) * CAP * wide)
+
+    @pl.when(jnp.logical_not(middle))
+    def _():
+        settle(y_send, (2 * zs - 2) * CAP * wide)
 
     @pl.loop(0, zs)
     def _(e):
         zi, out, j = place_of(e)
-        swap_y(zi, 1).wait_send()
-
-        @pl.when(out != ha)
+        split = is_late(zi, z, zs)
+
+        @pl.when((out != ha) & (e < zs - 1))
         def _():
             swap_yx(j, 1).wait_send()
 
-        behind = is_late(zi, z, zs)
-
-        @pl.when(behind)
-        def _():
-            swap_y(zi, 0).wait_send()
-
-            @pl.when(out != ha)
-            def _():
-                swap_yx(j, 0).wait_send()
-
-        @pl.when(jnp.logical_not(behind))
-        def _():
-            @pl.when(out != ha)
-            def _():
-                swap_x(j).wait_send()
-
-            @pl.when(out == ha)
-            def _():
-                swap_xy(j).wait_send()
-
-    for u in range(width // cut):
-        out_copy(u).wait()
+        @pl.when((out != ha) & (e < zs - 1) & split)
+        def _():
+            swap_yx(j, 0).wait_send()
+
+        @pl.when((out != ha) & (e == zs - 1))
+        def _():
+            for yy in (0, 1):
+                for c in (0, 1):
+                    swap_part_x(j, yy, c).wait_send()
+
+        @pl.when((out != ha) & jnp.logical_not(split))
+        def _():
+            swap_x(j).wait_send()
+
+        @pl.when((out == ha) & jnp.logical_not(split))
+        def _():
+            swap_xy(j).wait_send()
+
+    pltpu.make_async_copy(y_buf, y_ref, out_sem).wait()
 
 
 def expert(ids, keep, weight, tokens, gate, up, down):
@@ -550,7 +618,6 @@
     group = 4 * fd
     wide = 2 * fd
     any_spec = pl.BlockSpec(memory_space=pl.ANY)
-    vmem = pl.BlockSpec(memory_space=pltpu.VMEM)
     dma = pltpu.SemaphoreType.DMA
     bf16, f32 = jnp.bfloat16, jnp.float32
     return pl.pallas_call(
@@ -559,11 +626,12 @@
             jax.ShapeDtypeStruct((CAP, span * group), bf16), jax.ShapeDtypeStruct((1, tokens.shape[0]), jnp.int32)
         ),
         in_specs=[any_spec] * 7,
-        out_specs=(any_spec, vmem),
+        out_specs=(any_spec, any_spec),
         scratch_shapes=[
             pltpu.VMEM(ids.shape, jnp.int32),
             pltpu.VMEM(ids.shape, jnp.int32),
             pltpu.VMEM(ids.shape, f32),
+            pltpu.VMEM((1, tokens.shape[0]), jnp.int32),
             pltpu.VMEM((2, span, 2, 2, fd, q), bf16),
             pltpu.VMEM((zs, 2, 2, fd, q), bf16),
             pltpu.VMEM((3, fd, q), bf16),
@@ -579,24 +647,24 @@
             pltpu.VMEM((span, 2 * CAP, wide), f32),
             pltpu.VMEM((span, 2 * CAP, wide), bf16),
             pltpu.VMEM((span, 2 * CAP, wide), bf16),
-            pltpu.VMEM((2, zs, CAP, wide), f32),
-            pltpu.VMEM((2, zs, CAP, wide), bf16),
-            pltpu.VMEM((2, zs, CAP, wide), bf16),
+            pltpu.VMEM((2, zs, 2, CAP, fd), f32),
+            pltpu.VMEM((2, zs, 2, CAP, fd), bf16),
+            pltpu.VMEM((2, zs, 2, CAP, fd), bf16),
             pltpu.VMEM((span, CAP, wide), f32),
             pltpu.VMEM((span, CAP, wide), bf16),
             pltpu.VMEM((span, CAP, wide), bf16),
-            pltpu.VMEM((2, span, CAP, wide), bf16),
-            pltpu.VMEM((2, span, CAP, wide), bf16),
+            pltpu.VMEM((2, span, 2, CAP, fd), bf16),
+            pltpu.VMEM((2, span, 2, CAP, fd), bf16),
             pltpu.VMEM((CAP, 2 * span * wide), bf16),
             pltpu.VMEM((8, 128), jnp.int32),
             pltpu.VMEM((n, 8, 128), jnp.int32),
             pltpu.VMEM((CAP, 128), f32),
-            dma((3, 2)), dma((sub + span,)), dma((n,)), dma((n,)), dma((3,)), dma((3,)),
-            dma((2, 2, span, 2)), dma((2, span, 2)), dma((2, span, 2)), dma((2, span, 2)),
-            dma((2, 1, zs, 2)), dma((1, zs, 2)), dma((1, zs, 2)), dma((1, zs, 2)),
-            dma((6,)), dma((6,)), dma((2,)), dma((2,)),
-            dma((span,)), dma((span,)), dma((2, zs)), dma((2, zs)),
-            dma((span,)), dma((span,)), dma((2, span)), dma((2, span)), dma((2 * span,)), dma((3,)),
+            dma((3,)), dma((sub + span,)), dma((2,)), dma,
+            dma, dma((2, span, 2)), dma, dma((span,)),
+            dma, dma((1, zs, 2)), dma, dma((zs, 2)),
+            dma, dma((6,)), dma, dma((2,)),
+            dma((span,)), dma((span,)), dma, dma((2, zs)),
+            dma((span,)), dma((span,)), dma((2, span)), dma((2, span)), dma((2, 2)), dma((2, 2, 2)), dma, dma((4,)),
         ],
         compiler_params=pltpu.CompilerParams(
             collective_id=0, has_side_effects=True, vmem_limit_bytes=60 * 1024 * 1024
@@ -604,12 +672,47 @@
     )(ids, keep, weight, tokens, gate, up, down)
 
 
+def combine_kernel(place_ref, y_ref, out_ref, rows, block, in_sem, out_sem):
+    count, tokens, wide = block.shape
+    loads = [
+        pltpu.make_async_copy(y_ref.at[:, k * wide:(k + 1) * wide], rows.at[k], in_sem.at[k]) for k in range(count)
+    ]
+    for load in loads:
+        load.start()
+    slots = lax.broadcasted_iota(jnp.int32, (CAP, tokens), 0)
+    pick = jnp.where(place_ref[...] == slots, jnp.float32(1.0), jnp.float32(0.0)).astype(jnp.bfloat16).T
+    stores = []
+    for k in range(count):
+        loads[k].wait()
+        block[k] = jnp.dot(pick, rows[k], preferred_element_type=jnp.float32).astype(jnp.bfloat16)
+        stores.append(pltpu.make_async_copy(block.at[k], out_ref.at[:, k * wide:(k + 1) * wide], out_sem.at[k]))
+        stores[k].start()
+    for store in stores:
+        store.wait()
+
+
+def combine(place, y):
+    tokens, width = place.shape[1], y.shape[1]
+    wide = 512 if width % 512 == 0 else width
+    count = width // wide
+    any_spec = pl.BlockSpec(memory_space=pl.ANY)
+    dma = pltpu.SemaphoreType.DMA
+    return pl.pallas_call(
+        combine_kernel,
+        out_shape=jax.ShapeDtypeStruct((tokens, width), jnp.bfloat16),
+        in_specs=[pl.BlockSpec(memory_space=pltpu.VMEM), any_spec],
+        out_specs=any_spec,
+        scratch_shapes=[
+            pltpu.VMEM((count, CAP, wide), jnp.bfloat16),
+            pltpu.VMEM((count, tokens, wide), jnp.bfloat16),
+            dma((count,)), dma((count,)),
+        ],
+    )(place, y)
+
+
 def per_device(tokens, expert_ids, keep_mask, route_weight, gate_weight, up_weight, down_weight):
     y, place = expert(expert_ids.T, keep_mask.T, route_weight.T, tokens, gate_weight, up_weight, down_weight)
-    place = place[0]
-    slot_ids = jnp.arange(CAP, dtype=jnp.int32)
-    pick = (place[:, None] == slot_ids[None, :]).astype(jnp.bfloat16)
-    return jnp.dot(pick, y, preferred_element_type=jnp.float32).astype(jnp.bfloat16)
+    return combine(place, y)
 
 
 def solution(mesh):

time: 84.6 us -> 81.7 us (0.966)
  matrix products: 4.35 us -> 0 us
  Pallas kernels: 80.1 us -> 81.5 us
    dot_general x1 -> x0, matrix products: 4.35 us -> none  [per_device(): jnp.dot(pick, y, preferred_element_type=jnp.float32).astype(jnp.bfloat16)]
    pallas_call x0 -> x1, Pallas kernels: none -> 4.29 us  [combine(): pl.pallas_call(combine_kernel, out_shape=jax.ShapeDtypeStruct((tokens, wi...]
    pallas_call x1, Pallas kernels: 80.1 us -> 77.3 us  [expert(): pl.pallas_call(functools.partial(expert_kernel, n), out_shape=(jax.ShapeD...]
where the time goes in v4:
time: 81.7 us; the launch traced here: 81.6 us
  Pallas kernels  81.5 us (100%)
    pallas_call x1, Pallas kernels, expert(): pl.pallas_call(functools.partial(expert_kernel, n), out_shape=(jax.ShapeD...  77.3 us
    pallas_call x1, Pallas kernels, combine(): pl.pallas_call(combine_kernel, out_shape=jax.ShapeDtypeStruct((tokens, wi...  4.29 us

profile of v4, /device:TPU:3, one launch (start us, length us, event | category | flops | bytes accessed | tf_op | source)
XLA Modules:
  0.0 81.6 jit_solution(8924490192222627795)
XLA Ops:
  0.0 77.3 %shard_map.73 = (bf16[128,2048]{1,0:T(8,128)(2,1)}, s32[1,1024]{1,0:T(1,128)}) custom-call(s32[8,1024]{1,0:T(8,128)} %bitcast.3, s32[8,1024]{1,0:T(8,128)} %bitcast.4, f32[8,1024]{1,0:T(8,128)} %bitcast.5, bf16[1024,4096]{1,0:T(8,128)(2,1)} %tok_ref.1, bf16[256,768]{1,0:T(8,128)(2,1)} %gate_ref.1, bf16[256,768]{1,0:T(8,128)(2,1)} %up_ref.1, ...), custom_call_target="tpu_custom_call" | custom-call | tf_op jit(solution)/shard_map/pallas_call | solution.py:623
  77.3 4.3 %shard_map.74 = bf16[1024,2048]{1,0:T(8,128)(2,1)} custom-call(s32[1,1024]{1,0:T(1,128)} %get-tuple-element.7.place_ref, bf16[128,2048]{1,0:T(8,128)(2,1)} %get-tuple-element.8.y_ref), custom_call_target="tpu_custom_call" | custom-call | tf_op jit(solution)/shard_map/pallas_call | solution.py:700

commit v5 on v4

--- a/solution.py
+++ b/solution.py
@@ -60,10 +60,12 @@
         zi = low * zi + (1 - low) * (size - 1 - zi)
         return jnp.where(zi > 2 * at, zi, jnp.where(zi > at, 2 * (zi - at) - 1, 2 * (at - zi)))
 
-    def is_late(zi, at, size):
-        rank = rank_of(zi, at, size)
-        edge = (at == 0) | (at + 1 == size)
-        return (rank > size // 2) | (edge & ((rank == 1) | (rank > 2)))
+    def y_first(zi, yy):
+        rank = rank_of(zi, z, zs)
+        edge = (z == 0) | (z + 1 == zs)
+        if yy == 1:
+            return jnp.logical_not(edge & (rank == 2))
+        return (rank > span) | (edge & ((rank == 1) | (rank > 2)))
 
     def settle(sem, elements):
         rows = elements // group
@@ -333,8 +335,8 @@
         up = own_acc[1, yy * CAP:(yy + 1) * CAP] + part_in[yy, 1].astype(jnp.float32)
         hidden[yy] = (gate / (1.0 + jnp.exp(-gate)) * up).astype(jnp.bfloat16)
 
-    def swap_x(j):
-        return remote(x_out.at[j], x_in.at[j], x_send.at[j], x_recv.at[j], ha=1 - ha)
+    def swap_x(j, yy):
+        return remote(x_out.at[yy, j], x_in.at[yy, j], x_send.at[yy, j], x_recv.at[yy, j], ha=1 - ha)
 
     def swap_y(zi, yy):
         return remote(y_out.at[yy, zi], y_in.at[yy, zi], y_send, y_recv.at[yy, zi], wa=beside)
@@ -347,8 +349,8 @@
             yx_out.at[yy, j, c], yx_in.at[yy, j, c], part_send.at[yy, c], part_recv.at[1, yy, c], ha=1 - ha
         )
 
-    def swap_xy(j):
-        return remote(xy_out.at[j], xy_in.at[j], xy_send.at[j], xy_recv.at[j], wa=beside)
+    def swap_xy(j, yy):
+        return remote(xy_out.at[yy, j], xy_in.at[yy, j], xy_send.at[yy, j], xy_recv.at[yy, j], wa=beside)
 
     def swap_yx(j, yy):
         return remote(yx_out.at[yy, j], yx_in.at[yy, j], yx_send.at[yy, j], yx_recv.at[yy, j], ha=1 - ha)
@@ -367,19 +369,19 @@
         out = zi // span
         return zi, out, zi - out * span
 
-    def finish_x(e):
+    def finish_x(e, yy):
         zi, out, j = place_of(e)
-        second.given(0, zi, 0).wait_recv()
-        part = down(zi, 0)
+        second.given(0, zi, yy).wait_recv()
+        part = down(zi, yy)
 
         @pl.when(out == ha)
         def _():
-            x_own[j] = part
+            x_own[yy, j] = part
 
         @pl.when(out != ha)
         def _():
-            x_out[j] = part.astype(jnp.bfloat16)
-            swap_x(j).start()
+            x_out[yy, j] = part.astype(jnp.bfloat16)
+            swap_x(j, yy).start()
 
     def finish_y(e, yy):
         zi, out, j = place_of(e)
@@ -391,16 +393,16 @@
         for c in (0, 1):
             y_own[yy, zi, c] = keep[:, c * fd:(c + 1) * fd]
 
-    def combine_x(e):
+    def combine_x(e, yy):
         zi, out, j = place_of(e)
 
         @pl.when(out == ha)
         def _():
-            swap_x(j).wait_recv()
-            keep, leave = mine_rows(x_own[j] + x_in[j].astype(jnp.float32))
-            xy_own[j] = keep
-            xy_out[j] = leave.astype(jnp.bfloat16)
-            swap_xy(j).start()
+            swap_x(j, yy).wait_recv()
+            keep, leave = mine_rows(x_own[yy, j] + x_in[yy, j].astype(jnp.float32))
+            xy_own[yy, j] = keep
+            xy_out[yy, j] = leave.astype(jnp.bfloat16)
+            swap_xy(j, yy).start()
 
     def combine_y(e, yy):
         zi, out, j = place_of(e)
@@ -416,19 +418,23 @@
         def _():
             y_own[yy, zi] = total
 
-    def finish_last(yy):
+    def part_last(yy, c):
         zi, out, j = place_of(zs - 1)
-        second.serve(0, zi, yy)
-        for c in (core, 1 - core):
-            if c is not core:
-                second.given(0, zi, yy).wait_recv()
-            keep, leave = mine_rows(lax.dot_general(
-                hidden[...].reshape(2 * CAP, q), w2[zi, yy, c], (((1,), (1,)), ((), ())),
-                preferred_element_type=jnp.float32,
-            ))
-            y_out[yy, zi, c] = leave.astype(jnp.bfloat16)
-            swap_part(zi, yy, c).start()
-            y_own[yy, zi, c] = keep
+        keep, leave = mine_rows(lax.dot_general(
+            hidden[...].reshape(2 * CAP, q), w2[zi, yy, c], (((1,), (1,)), ((), ())),
+            preferred_element_type=jnp.float32,
+        ))
+        y_out[yy, zi, c] = leave.astype(jnp.bfloat16)
+        swap_part(zi, yy, c).start()
+        y_own[yy, zi, c] = keep
+
+    def start_last(yy):
+        second.serve(0, order(zs - 1, z, zs), yy)
+        part_last(yy, core)
+
+    def end_last(yy):
+        second.given(0, order(zs - 1, z, zs), yy).wait_recv()
+        part_last(yy, 1 - core)
 
     def combine_last(yy):
         zi, out, j = place_of(zs - 1)
@@ -453,7 +459,7 @@
     def _():
         @pl.loop(0, span + 1)
         def _(e):
-            finish_x(e)
+            finish_x(e, 0)
             finish_y(e, 1)
 
         @pl.loop(span + 1, zs - 1)
@@ -461,13 +467,15 @@
             late(e, 0)
             late(e, 1)
 
-        finish_last(0)
-        finish_last(1)
+        start_last(0)
+        end_last(0)
+        start_last(1)
+        end_last(1)
 
         @pl.loop(0, span + 1)
         def _(e):
             combine_y(e, 1)
-            combine_x(e)
+            combine_x(e, 0)
 
         @pl.loop(span + 1, zs - 1)
         def _(e):
@@ -480,14 +488,14 @@
     @pl.when(jnp.logical_not(middle))
     def _():
         finish_y(0, 1)
-        finish_x(0)
+        finish_x(0, 0)
         finish_y(1, 0)
         finish_y(1, 1)
         second.serve(0, order(2, z, zs), 0)
-        finish_x(2)
-        late(2, 1)
+        finish_x(2, 0)
+        second.serve(0, order(2, z, zs), 1)
+        finish_x(2, 1)
         combine_y(0, 1)
-        combine_x(0)
         combine_y(1, 0)
 
         @pl.loop(3, zs - 1)
@@ -497,13 +505,16 @@
             combine_y(e, 0)
             combine_y(e, 1)
 
-        finish_last(0)
+        start_last(0)
         combine_y(1, 1)
-        combine_y(2, 1)
-        combine_x(2)
-        finish_last(1)
+        end_last(0)
+        combine_x(2, 0)
+        start_last(1)
+        end_last(1)
+        combine_x(0, 0)
         combine_last(0)
         combine_last(1)
+        combine_x(2, 1)
 
     all_counts().wait_recv()
 
@@ -534,7 +545,7 @@
             zi = ha * span + j
             u = 2 * j + yy
             final = rank_of(zi, z, zs) == zs - 1
-            split = is_late(zi, z, zs) if yy == 0 else final | True
+            split = y_first(zi, yy)
 
             @pl.when(final)
             def _():
@@ -549,11 +560,10 @@
             def _():
                 put_y(u, zi, yy, j)
 
-            if yy == 0:
-                @pl.when(jnp.logical_not(split))
-                def _():
-                    swap_xy(j).wait_recv()
-                    put(u, xy_own[j] + xy_in[j].astype(jnp.float32))
+            @pl.when(jnp.logical_not(split))
+            def _():
+                swap_xy(j, yy).wait_recv()
+                put(u, xy_own[yy, j] + xy_in[yy, j].astype(jnp.float32))
 
             if cut == wide:
                 out_copy(u).start()
@@ -576,34 +586,30 @@
 
     @pl.when(jnp.logical_not(middle))
     def _():
-        settle(y_send, (2 * zs - 2) * CAP * wide)
+        settle(y_send, (2 * zs - 3) * CAP * wide)
 
     @pl.loop(0, zs)
     def _(e):
         zi, out, j = place_of(e)
-        split = is_late(zi, z, zs)
-
-        @pl.when((out != ha) & (e < zs - 1))
-        def _():
-            swap_yx(j, 1).wait_send()
-
-        @pl.when((out != ha) & (e < zs - 1) & split)
-        def _():
-            swap_yx(j, 0).wait_send()
-
-        @pl.when((out != ha) & (e == zs - 1))
-        def _():
-            for yy in (0, 1):
+        for yy in (0, 1):
+            split = y_first(zi, yy)
+
+            @pl.when((out != ha) & (e < zs - 1) & split)
+            def _():
+                swap_yx(j, yy).wait_send()
+
+            @pl.when((out != ha) & (e == zs - 1))
+            def _():
                 for c in (0, 1):
                     swap_part_x(j, yy, c).wait_send()
 
-        @pl.when((out != ha) & jnp.logical_not(split))
-        def _():
-            swap_x(j).wait_send()
-
-        @pl.when((out == ha) & jnp.logical_not(split))
-        def _():
-            swap_xy(j).wait_send()
+            @pl.when((out != ha) & jnp.logical_not(split))
+            def _():
+                swap_x(j, yy).wait_send()
+
+            @pl.when((out == ha) & jnp.logical_not(split))
+            def _():
+                swap_xy(j, yy).wait_send()
 
     pltpu.make_async_copy(y_buf, y_ref, out_sem).wait()
 
@@ -644,15 +650,15 @@
             pltpu.VMEM((2, 2, CAP, q), bf16),
             pltpu.VMEM((2, 2, CAP, q), bf16),
             pltpu.VMEM((2, CAP, q), bf16),
-            pltpu.VMEM((span, 2 * CAP, wide), f32),
-            pltpu.VMEM((span, 2 * CAP, wide), bf16),
-            pltpu.VMEM((span, 2 * CAP, wide), bf16),
+            pltpu.VMEM((2, span, 2 * CAP, wide), f32),
+            pltpu.VMEM((2, span, 2 * CAP, wide), bf16),
+            pltpu.VMEM((2, span, 2 * CAP, wide), bf16),
             pltpu.VMEM((2, zs, 2, CAP, fd), f32),
             pltpu.VMEM((2, zs, 2, CAP, fd), bf16),
             pltpu.VMEM((2, zs, 2, CAP, fd), bf16),
-            pltpu.VMEM((span, CAP, wide), f32),
-            pltpu.VMEM((span, CAP, wide), bf16),
-            pltpu.VMEM((span, CAP, wide), bf16),
+            pltpu.VMEM((2, span, CAP, wide), f32),
+            pltpu.VMEM((2, span, CAP, wide), bf16),
+            pltpu.VMEM((2, span, CAP, wide), bf16),
             pltpu.VMEM((2, span, 2, CAP, fd), bf16),
             pltpu.VMEM((2, span, 2, CAP, fd), bf16),
             pltpu.VMEM((CAP, 2 * span * wide), bf16),
@@ -663,8 +669,8 @@
             dma, dma((2, span, 2)), dma, dma((span,)),
             dma, dma((1, zs, 2)), dma, dma((zs, 2)),
             dma, dma((6,)), dma, dma((2,)),
-            dma((span,)), dma((span,)), dma, dma((2, zs)),
-            dma((span,)), dma((span,)), dma((2, span)), dma((2, span)), dma((2, 2)), dma((2, 2, 2)), dma, dma((4,)),
+            dma((2, span)), dma((2, span)), dma, dma((2, zs)),
+            dma((2, span)), dma((2, span)), dma((2, span)), dma((2, span)), dma((2, 2)), dma((2, 2, 2)), dma, dma((4,)),
         ],
         compiler_params=pltpu.CompilerParams(
             collective_id=0, has_side_effects=True, vmem_limit_bytes=60 * 1024 * 1024
@@ -672,21 +678,27 @@
     )(ids, keep, weight, tokens, gate, up, down)
 
 
-def combine_kernel(place_ref, y_ref, out_ref, rows, block, in_sem, out_sem):
-    count, tokens, wide = block.shape
-    loads = [
-        pltpu.make_async_copy(y_ref.at[:, k * wide:(k + 1) * wide], rows.at[k], in_sem.at[k]) for k in range(count)
-    ]
+def combine_kernel(place_ref, y_ref, out_ref, place, rows, block, in_sem, out_sem):
+    steps, tall, _ = block.shape
+    count, _, wide = rows.shape
+    loads = [pltpu.make_async_copy(place_ref, place, in_sem.at[count])]
+    for k in range(count):
+        loads.append(pltpu.make_async_copy(y_ref.at[:, k * wide:(k + 1) * wide], rows.at[k], in_sem.at[k]))
     for load in loads:
         load.start()
-    slots = lax.broadcasted_iota(jnp.int32, (CAP, tokens), 0)
-    pick = jnp.where(place_ref[...] == slots, jnp.float32(1.0), jnp.float32(0.0)).astype(jnp.bfloat16).T
+    loads[0].wait()
+    slots = lax.broadcasted_iota(jnp.int32, (CAP, steps * tall), 0)
+    pick = jnp.where(place[...] == slots, jnp.float32(1.0), jnp.float32(0.0)).astype(jnp.bfloat16).T
+    for load in loads[1:]:
+        load.wait()
     stores = []
-    for k in range(count):
-        loads[k].wait()
-        block[k] = jnp.dot(pick, rows[k], preferred_element_type=jnp.float32).astype(jnp.bfloat16)
-        stores.append(pltpu.make_async_copy(block.at[k], out_ref.at[:, k * wide:(k + 1) * wide], out_sem.at[k]))
-        stores[k].start()
+    for i in range(steps):
+        for k in range(count):
+            block[i, :, k * wide:(k + 1) * wide] = jnp.dot(
+                pick[i * tall:(i + 1) * tall], rows[k], preferred_element_type=jnp.float32
+            ).astype(jnp.bfloat16)
+        stores.append(pltpu.make_async_copy(block.at[i], out_ref.at[i * tall:(i + 1) * tall], out_sem.at[i]))
+        stores[i].start()
     for store in stores:
         store.wait()
 
@@ -694,18 +706,20 @@
 def combine(place, y):
     tokens, width = place.shape[1], y.shape[1]
     wide = 512 if width % 512 == 0 else width
-    count = width // wide
+    tall = CAP if tokens % CAP == 0 else tokens
+    count, steps = width // wide, tokens // tall
     any_spec = pl.BlockSpec(memory_space=pl.ANY)
     dma = pltpu.SemaphoreType.DMA
     return pl.pallas_call(
         combine_kernel,
         out_shape=jax.ShapeDtypeStruct((tokens, width), jnp.bfloat16),
-        in_specs=[pl.BlockSpec(memory_space=pltpu.VMEM), any_spec],
+        in_specs=[any_spec, any_spec],
         out_specs=any_spec,
         scratch_shapes=[
+            pltpu.VMEM((1, tokens), jnp.int32),
             pltpu.VMEM((count, CAP, wide), jnp.bfloat16),
-            pltpu.VMEM((count, tokens, wide), jnp.bfloat16),
-            dma((count,)), dma((count,)),
+            pltpu.VMEM((steps, tall, width), jnp.bfloat16),
+            dma((count + 1,)), dma((steps,)),
         ],
     )(place, y)
 

time: 81.7 us -> 80 us (0.979); the launches traced: 81.6 us -> 78.9 us
  Pallas kernels: 81.5 us -> 78.9 us
    pallas_call x1, Pallas kernels: 77.3 us -> 75.4 us  [expert(): pl.pallas_call(functools.partial(expert_kernel, n), out_shape=(jax.ShapeD...]
where the time goes in v5:
time: 80 us; the launch traced here: 78.9 us
  Pallas kernels  78.9 us (99%)
    pallas_call x1, Pallas kernels, expert(): pl.pallas_call(functools.partial(expert_kernel, n), out_shape=(jax.ShapeD...  75.4 us
    pallas_call x1, Pallas kernels, combine(): pl.pallas_call(combine_kernel, out_shape=jax.ShapeDtypeStruct((tokens, wi...  3.5 us

profile of v5, /device:TPU:3, one launch (start us, length us, event | category | flops | bytes accessed | tf_op | source)
XLA Modules:
  0.0 78.9 jit_solution(4223110730123874442)
XLA Ops:
  0.0 75.4 %shard_map.73 = (bf16[128,2048]{1,0:T(8,128)(2,1)}, s32[1,1024]{1,0:T(1,128)}) custom-call(s32[8,1024]{1,0:T(8,128)} %bitcast.3, s32[8,1024]{1,0:T(8,128)} %bitcast.4, f32[8,1024]{1,0:T(8,128)} %bitcast.5, bf16[1024,4096]{1,0:T(8,128)(2,1)} %tok_ref.1, bf16[256,768]{1,0:T(8,128)(2,1)} %gate_ref.1, bf16[256,768]{1,0:T(8,128)(2,1)} %up_ref.1, ...), custom_call_target="tpu_custom_call" | custom-call | tf_op jit(solution)/shard_map/pallas_call | solution.py:629
  75.4 3.5 %shard_map.74 = bf16[1024,2048]{1,0:T(8,128)(2,1)} custom-call(s32[1,1024]{1,0:T(1,128)} %get-tuple-element.7.place_ref, bf16[128,2048]{1,0:T(8,128)(2,1)} %get-tuple-element.8.y_ref), custom_call_target="tpu_custom_call" | custom-call | tf_op jit(solution)/shard_map/pallas_call | solution.py:713

commit v6 on v5

--- a/solution.py
+++ b/solution.py
@@ -15,11 +15,11 @@
     n,
     ids_ref, keep_ref, route_ref, tok_ref, gate_ref, up_ref, down_ref,
     y_ref, place_ref,
-    ids, keep, weight, place_buf, w1, w2, stage, tok_buf, guest_out, own_rows, guest_rows, own_acc, guest_acc, part_out, part_in, hidden,
+    ids, keep, weight, place_buf, w1, w2, stage, tok_buf, guest_out, own_rows, guest_rows, own_acc, part_out, part_in, hidden,
     x_own, x_out, x_in, y_own, y_out, y_in, xy_own, xy_out, xy_in, yx_out, yx_in, y_buf, count, counts, route,
     load_sem, tok_sem, c_sem, e_send, l1_send, l1_recv, b1_send, b1_recv, l2_send, l2_recv, b2_send, b2_recv,
-    g_send, g_recv, p_send, p_recv, x_send, x_recv, y_send, y_recv, xy_send, xy_recv, yx_send, yx_recv,
-    part_send, part_recv, out_sem, route_sem,
+    g_send, g_recv, p_send, p_recv, x_recv, y_send, y_recv, xy_recv, yx_recv,
+    part_recv, out_sem, route_sem,
 ):
     zs = n // 4
     span = zs // 2
@@ -64,7 +64,7 @@
         rank = rank_of(zi, z, zs)
         edge = (z == 0) | (z + 1 == zs)
         if yy == 1:
-            return jnp.logical_not(edge & (rank == 2))
+            return rank >= 0
         return (rank > span) | (edge & ((rank == 1) | (rank > 2)))
 
     def settle(sem, elements):
@@ -128,7 +128,7 @@
 
             settle(self.b_send, self.size * unit)
 
-    first = Line(lambda c, t, zi, yy: w1.at[t, zi, yy, c], zl, span, (l1_send, l1_recv, b1_send, lambda t, zi, yy: b1_recv.at[zi]))
+    first = Line(lambda c, t, zi, yy: w1.at[t, zi, yy, c], zl, span, (l1_send, l1_recv, b1_send, lambda t, zi, yy: b1_recv.at[t, zi]))
     second = Line(lambda c, t, zi, yy: w2.at[zi, yy, c], z, zs, (l2_send, l2_recv, b2_send, lambda t, zi, yy: b2_recv.at[zi, yy]))
 
     def exchange(t):
@@ -201,15 +201,9 @@
     own_y, own_y_got = direct(own_rows, y, g_sems, 4, **to_y), direct(own_rows, 1 - y, g_sems, 4, **to_y)
     own_d, own_d_got = direct(own_rows, 1 - y, g_sems, 5, **to_x), other(own_rows, 1 - y, g_sems, 5, **to_x)
 
-    def line_in(e):
+    def given_all(t, e):
         zi = order(e, zl, span)
-        for yy in (y, 1 - y):
-            for t in (0, 1):
-                first.serve(t, zi, yy)
-
-    def line_all(e):
-        zi = order(e, zl, span)
-        same(w1.at[:, zi, :, 1 - core], b1_send, b1_recv.at[zi], wa=sibling).wait_recv()
+        same(w1.at[t, zi, :, 1 - core], b1_send, b1_recv.at[t, zi], wa=sibling).wait_recv()
 
     def line2_in(e):
         zi = order(e, z, zs)
@@ -226,8 +220,16 @@
     def mine(zi):
         return own_rows[zi].reshape(2 * CAP, group)
 
-    def partial(yy):
-        return remote(part_out.at[yy], part_in.at[yy], p_send, p_recv.at[yy], wa=mirror)
+    def partial(yy, t):
+        return remote(part_out.at[yy, t], part_in.at[yy, t], p_send, p_recv.at[yy, t], wa=mirror)
+
+    def serve_guest(yy, t):
+        total = None
+        for e in range(span):
+            term = project(guests(yy), e, t)
+            total = term if total is None else total + term
+        part_out[yy, t] = total.astype(jnp.bfloat16)
+        partial(yy, t).start()
 
     loaded(0)
     exchange(0).start()
@@ -281,21 +283,22 @@
     guest_x.start()
     own_y.start()
     second.serve(0, z, 1 - y)
-    line_all(0)
+    for t in (0, 1):
+        given_all(t, 0)
     guest_y_got.wait_recv()
     guest_d.start()
     guest_x_got.wait_recv()
-    for t in (0, 1):
-        guest_acc[t] = project(guests(y), 0, t)
     for e in range(1, span):
-        line_in(e)
-        line_all(e)
-        if e + 1 < span:
-            for t in (0, 1):
-                guest_acc[t] = guest_acc[t] + project(guests(y), e, t)
-    for t in (0, 1):
-        part_out[y, t] = (guest_acc[t] + project(guests(y), span - 1, t)).astype(jnp.bfloat16)
-    partial(y).start()
+        zi = order(e, zl, span)
+        for t in (0, 1):
+            first.serve(t, zi, y)
+        first.serve(0, zi, 1 - y)
+        given_all(0, e)
+    serve_guest(y, 0)
+    for e in range(1, span):
+        first.serve(1, order(e, zl, span), 1 - y)
+        given_all(1, e)
+    serve_guest(y, 1)
     middle = (z > 0) & (z + 1 < zs)
 
     @pl.when(middle)
@@ -306,11 +309,7 @@
     own_d.start()
     guest_d_got.wait_recv()
     for t in (0, 1):
-        total = project(guests(1 - y), 0, t)
-        for e in range(1, span):
-            total = total + project(guests(1 - y), e, t)
-        part_out[1 - y, t] = total.astype(jnp.bfloat16)
-    partial(1 - y).start()
+        serve_guest(1 - y, t)
 
     @pl.when(jnp.logical_not(middle))
     def _():
@@ -329,14 +328,15 @@
             total = total + project(mine, e, t)
         own_acc[t] = total
     for yy in (0, 1):
-        partial(yy).wait_recv()
+        for t in (0, 1):
+            partial(yy, t).wait_recv()
     for yy in (0, 1):
         gate = own_acc[0, yy * CAP:(yy + 1) * CAP] + part_in[yy, 0].astype(jnp.float32)
         up = own_acc[1, yy * CAP:(yy + 1) * CAP] + part_in[yy, 1].astype(jnp.float32)
         hidden[yy] = (gate / (1.0 + jnp.exp(-gate)) * up).astype(jnp.bfloat16)
 
     def swap_x(j, yy):
-        return remote(x_out.at[yy, j], x_in.at[yy, j], x_send.at[yy, j], x_recv.at[yy, j], ha=1 - ha)
+        return remote(x_out.at[yy, j], x_in.at[yy, j], y_send, x_recv.at[yy, j], ha=1 - ha)
 
     def swap_y(zi, yy):
         return remote(y_out.at[yy, zi], y_in.at[yy, zi], y_send, y_recv.at[yy, zi], wa=beside)
@@ -346,14 +346,14 @@
 
     def swap_part_x(j, yy, c):
         return remote(
-            yx_out.at[yy, j, c], yx_in.at[yy, j, c], part_send.at[yy, c], part_recv.at[1, yy, c], ha=1 - ha
+            yx_out.at[yy, j, c], yx_in.at[yy, j, c], y_send, part_recv.at[1, yy, c], ha=1 - ha
         )
 
     def swap_xy(j, yy):
-        return remote(xy_out.at[yy, j], xy_in.at[yy, j], xy_send.at[yy, j], xy_recv.at[yy, j], wa=beside)
+        return remote(xy_out.at[yy, j], xy_in.at[yy, j], y_send, xy_recv.at[yy, j], wa=beside)
 
     def swap_yx(j, yy):
-        return remote(yx_out.at[yy, j], yx_in.at[yy, j], yx_send.at[yy, j], yx_recv.at[yy, j], ha=1 - ha)
+        return remote(yx_out.at[yy, j], yx_in.at[yy, j], y_send, yx_recv.at[yy, j], ha=1 - ha)
 
     def mine_rows(v):
         return jnp.where(y == 0, v[:CAP], v[CAP:]), jnp.where(y == 0, v[CAP:], v[:CAP])
@@ -493,8 +493,7 @@
         finish_y(1, 1)
         second.serve(0, order(2, z, zs), 0)
         finish_x(2, 0)
-        second.serve(0, order(2, z, zs), 1)
-        finish_x(2, 1)
+        late(2, 1)
         combine_y(0, 1)
         combine_y(1, 0)
 
@@ -509,12 +508,12 @@
         combine_y(1, 1)
         end_last(0)
         combine_x(2, 0)
+        combine_y(2, 1)
         start_last(1)
         end_last(1)
         combine_x(0, 0)
         combine_last(0)
         combine_last(1)
-        combine_x(2, 1)
 
     all_counts().wait_recv()
 
@@ -580,36 +579,15 @@
     first.drain(2)
     second.drain(1)
 
+    unit = CAP * wide
+
     @pl.when(middle)
     def _():
-        settle(y_send, (zs + zs - 1 - span) * CAP * wide)
+        settle(y_send, (2 * span + span + 1 + 2 * zs - 1 - span) * unit)
 
     @pl.when(jnp.logical_not(middle))
     def _():
-        settle(y_send, (2 * zs - 3) * CAP * wide)
-
-    @pl.loop(0, zs)
-    def _(e):
-        zi, out, j = place_of(e)
-        for yy in (0, 1):
-            split = y_first(zi, yy)
-
-            @pl.when((out != ha) & (e < zs - 1) & split)
-            def _():
-                swap_yx(j, yy).wait_send()
-
-            @pl.when((out != ha) & (e == zs - 1))
-            def _():
-                for c in (0, 1):
-                    swap_part_x(j, yy, c).wait_send()
-
-            @pl.when((out != ha) & jnp.logical_not(split))
-            def _():
-                swap_x(j, yy).wait_send()
-
-            @pl.when((out == ha) & jnp.logical_not(split))
-            def _():
-                swap_xy(j, yy).wait_send()
+        settle(y_send, (2 * span + 2 * zs) * unit)
 
     pltpu.make_async_copy(y_buf, y_ref, out_sem).wait()
 
@@ -646,7 +624,6 @@
             pltpu.VMEM((span, 2, CAP, group), bf16),
             pltpu.VMEM((span, 2, CAP, group), bf16),
             pltpu.VMEM((2, 2 * CAP, q), f32),
-            pltpu.VMEM((2, CAP, q), f32),
             pltpu.VMEM((2, 2, CAP, q), bf16),
             pltpu.VMEM((2, 2, CAP, q), bf16),
             pltpu.VMEM((2, CAP, q), bf16),
@@ -666,11 +643,10 @@
             pltpu.VMEM((n, 8, 128), jnp.int32),
             pltpu.VMEM((CAP, 128), f32),
             dma((3,)), dma((sub + span,)), dma((2,)), dma,
-            dma, dma((2, span, 2)), dma, dma((span,)),
+            dma, dma((2, span, 2)), dma, dma((2, span)),
             dma, dma((1, zs, 2)), dma, dma((zs, 2)),
-            dma, dma((6,)), dma, dma((2,)),
-            dma((2, span)), dma((2, span)), dma, dma((2, zs)),
-            dma((2, span)), dma((2, span)), dma((2, span)), dma((2, span)), dma((2, 2)), dma((2, 2, 2)), dma, dma((4,)),
+            dma, dma((6,)), dma, dma((2, 2)),
+            dma((2, span)), dma, dma((2, zs)), dma((2, span)), dma((2, span)), dma((2, 2, 2)), dma, dma((4,)),
         ],
         compiler_params=pltpu.CompilerParams(
             collective_id=0, has_side_effects=True, vmem_limit_bytes=60 * 1024 * 1024

time: 80 us -> 77.6 us (0.970)
  Pallas kernels: 78.9 us -> 77.3 us
    pallas_call x1, Pallas kernels: 75.4 us -> 73.8 us  [expert(): pl.pallas_call(functools.partial(expert_kernel, n), out_shape=(jax.ShapeD...]
where the time goes in v6:
time: 77.6 us; the launch traced here: 77.3 us
  Pallas kernels  77.3 us (100%)
    pallas_call x1, Pallas kernels, expert(): pl.pallas_call(functools.partial(expert_kernel, n), out_shape=(jax.ShapeD...  73.8 us
    pallas_call x1, Pallas kernels, combine(): pl.pallas_call(combine_kernel, out_shape=jax.ShapeDtypeStruct((tokens, wi...  3.5 us

profile of v6, /device:TPU:3, one launch (start us, length us, event | category | flops | bytes accessed | tf_op | source)
XLA Modules:
  0.0 77.3 jit_solution(16415615262914031635)
XLA Ops:
  0.0 73.8 %shard_map.73 = (bf16[128,2048]{1,0:T(8,128)(2,1)}, s32[1,1024]{1,0:T(1,128)}) custom-call(s32[8,1024]{1,0:T(8,128)} %bitcast.3, s32[8,1024]{1,0:T(8,128)} %bitcast.4, f32[8,1024]{1,0:T(8,128)} %bitcast.5, bf16[1024,4096]{1,0:T(8,128)(2,1)} %tok_ref.1, bf16[256,768]{1,0:T(8,128)(2,1)} %gate_ref.1, bf16[256,768]{1,0:T(8,128)(2,1)} %up_ref.1, ...), custom_call_target="tpu_custom_call" | custom-call | tf_op jit(solution)/shard_map/pallas_call | solution.py:607
  73.8 3.5 %shard_map.74 = bf16[1024,2048]{1,0:T(8,128)(2,1)} custom-call(s32[1,1024]{1,0:T(1,128)} %get-tuple-element.7.place_ref, bf16[128,2048]{1,0:T(8,128)(2,1)} %get-tuple-element.8.y_ref), custom_call_target="tpu_custom_call" | custom-call | tf_op jit(solution)/shard_map/pallas_call | solution.py:689

commit v7 on v6

--- a/solution.py
+++ b/solution.py
@@ -15,11 +15,11 @@
     n,
     ids_ref, keep_ref, route_ref, tok_ref, gate_ref, up_ref, down_ref,
     y_ref, place_ref,
-    ids, keep, weight, place_buf, w1, w2, stage, tok_buf, guest_out, own_rows, guest_rows, own_acc, part_out, part_in, hidden,
-    x_own, x_out, x_in, y_own, y_out, y_in, xy_own, xy_out, xy_in, yx_out, yx_in, y_buf, count, counts, route,
+    ids, keep, weight, w1, w2, stage, tok_buf, guest_out, own_rows, guest_rows, own_acc, part_out, part_in, hidden,
+    x_own, x_out, x_in, y_own, y_out, y_in, xy_own, xy_out, xy_in, yx_out, yx_in, count, counts, route,
     load_sem, tok_sem, c_sem, e_send, l1_send, l1_recv, b1_send, b1_recv, l2_send, l2_recv, b2_send, b2_recv,
     g_send, g_recv, p_send, p_recv, x_recv, y_send, y_recv, xy_recv, yx_recv,
-    part_recv, out_sem, route_sem,
+    part_recv, route_sem,
 ):
     zs = n // 4
     span = zs // 2
@@ -247,9 +247,7 @@
         running = running + jnp.where(lane >= shift, pltpu.roll(running, shift, 1), 0)
         shift *= 2
     place = jnp.where(chosen == 1, running[0:1] - 1, -1)
-    place_buf[...] = place
-    place_copy = pltpu.make_async_copy(place_buf, place_ref, route_sem.at[3])
-    place_copy.start()
+    place_ref[...] = place
     count[...] = jnp.broadcast_to(jnp.sum(chosen, axis=1, keepdims=True), count.shape)
     slot_ids = lax.broadcasted_iota(jnp.int32, (CAP, length), 0)
     hit = place == slot_ids
@@ -525,19 +523,13 @@
     earlier = lax.fori_loop(0, n, add_count, jnp.zeros(counts.shape[1:], jnp.int32))
     slot = lax.broadcasted_iota(jnp.int32, (CAP, 1), 0)
     scale = jnp.where(slot + earlier[0:1, 0:1] < n // 2 * CAP, route[:, 0:1], jnp.float32(0.0))
-    width = 2 * span * wide
-    cut = wide if wide % 128 == 0 else width
-
-    def out_copy(u):
-        return pltpu.make_async_copy(y_buf.at[:, u * cut:(u + 1) * cut], y_ref.at[:, u * cut:(u + 1) * cut], out_sem)
-
     def put(u, total):
-        y_buf[:, u * wide:(u + 1) * wide] = (total * scale).astype(jnp.bfloat16)
+        y_ref[:, u * wide:(u + 1) * wide] = (total * scale).astype(jnp.bfloat16)
 
     def put_y(u, zi, yy, j):
         for c in (0, 1):
             total = y_own[yy, zi, c] + yx_in[yy, j, c].astype(jnp.float32)
-            y_buf[:, u * wide + c * fd:u * wide + (c + 1) * fd] = (total * scale).astype(jnp.bfloat16)
+            y_ref[:, u * wide + c * fd:u * wide + (c + 1) * fd] = (total * scale).astype(jnp.bfloat16)
 
     for yy in (1, 0):
         for j in range(span):
@@ -564,15 +556,8 @@
                 swap_xy(j, yy).wait_recv()
                 put(u, xy_own[yy, j] + xy_in[yy, j].astype(jnp.float32))
 
-            if cut == wide:
-                out_copy(u).start()
-
-    if cut != wide:
-        out_copy(0).start()
-
     all_counts().wait_send()
 
-    place_copy.wait()
     settle(e_send, 3 * fd * q)
     settle(g_send, 6 * sub * CAP * group)
     settle(p_send, 4 * CAP * q)
@@ -588,8 +573,6 @@
     @pl.when(jnp.logical_not(middle))
     def _():
         settle(y_send, (2 * span + 2 * zs) * unit)
-
-    pltpu.make_async_copy(y_buf, y_ref, out_sem).wait()
 
 
 def expert(ids, keep, weight, tokens, gate, up, down):
@@ -602,20 +585,20 @@
     group = 4 * fd
     wide = 2 * fd
     any_spec = pl.BlockSpec(memory_space=pl.ANY)
+    vmem = pl.BlockSpec(memory_space=pltpu.VMEM)
     dma = pltpu.SemaphoreType.DMA
     bf16, f32 = jnp.bfloat16, jnp.float32
     return pl.pallas_call(
         functools.partial(expert_kernel, n),
         out_shape=(
-            jax.ShapeDtypeStruct((CAP, span * group), bf16), jax.ShapeDtypeStruct((1, tokens.shape[0]), jnp.int32)
+            pltpu.VMEM((CAP, span * group), bf16), pltpu.VMEM((1, tokens.shape[0]), jnp.int32)
         ),
         in_specs=[any_spec] * 7,
-        out_specs=(any_spec, any_spec),
+        out_specs=(vmem, vmem),
         scratch_shapes=[
             pltpu.VMEM(ids.shape, jnp.int32),
             pltpu.VMEM(ids.shape, jnp.int32),
             pltpu.VMEM(ids.shape, f32),
-            pltpu.VMEM((1, tokens.shape[0]), jnp.int32),
             pltpu.VMEM((2, span, 2, 2, fd, q), bf16),
             pltpu.VMEM((zs, 2, 2, fd, q), bf16),
             pltpu.VMEM((3, fd, q), bf16),
@@ -638,7 +621,6 @@
             pltpu.VMEM((2, span, CAP, wide), bf16),
             pltpu.VMEM((2, span, 2, CAP, fd), bf16),
             pltpu.VMEM((2, span, 2, CAP, fd), bf16),
-            pltpu.VMEM((CAP, 2 * span * wide), bf16),
             pltpu.VMEM((8, 128), jnp.int32),
             pltpu.VMEM((n, 8, 128), jnp.int32),
             pltpu.VMEM((CAP, 128), f32),
@@ -646,7 +628,7 @@
             dma, dma((2, span, 2)), dma, dma((2, span)),
             dma, dma((1, zs, 2)), dma, dma((zs, 2)),
             dma, dma((6,)), dma, dma((2, 2)),
-            dma((2, span)), dma, dma((2, zs)), dma((2, span)), dma((2, span)), dma((2, 2, 2)), dma, dma((4,)),
+            dma((2, span)), dma, dma((2, zs)), dma((2, span)), dma((2, span)), dma((2, 2, 2)), dma((3,)),
         ],
         compiler_params=pltpu.CompilerParams(
             collective_id=0, has_side_effects=True, vmem_limit_bytes=60 * 1024 * 1024
@@ -654,24 +636,16 @@
     )(ids, keep, weight, tokens, gate, up, down)
 
 
-def combine_kernel(place_ref, y_ref, out_ref, place, rows, block, in_sem, out_sem):
-    steps, tall, _ = block.shape
-    count, _, wide = rows.shape
-    loads = [pltpu.make_async_copy(place_ref, place, in_sem.at[count])]
-    for k in range(count):
-        loads.append(pltpu.make_async_copy(y_ref.at[:, k * wide:(k + 1) * wide], rows.at[k], in_sem.at[k]))
-    for load in loads:
-        load.start()
-    loads[0].wait()
+def combine_kernel(place_ref, y_ref, out_ref, block, out_sem):
+    steps, tall, width = block.shape
+    wide = 512 if width % 512 == 0 else width
     slots = lax.broadcasted_iota(jnp.int32, (CAP, steps * tall), 0)
-    pick = jnp.where(place[...] == slots, jnp.float32(1.0), jnp.float32(0.0)).astype(jnp.bfloat16).T
-    for load in loads[1:]:
-        load.wait()
+    pick = jnp.where(place_ref[...] == slots, jnp.float32(1.0), jnp.float32(0.0)).astype(jnp.bfloat16).T
     stores = []
     for i in range(steps):
-        for k in range(count):
-            block[i, :, k * wide:(k + 1) * wide] = jnp.dot(
-                pick[i * tall:(i + 1) * tall], rows[k], preferred_element_type=jnp.float32
+        for k in range(0, width, wide):
+            block[i, :, k:k + wide] = jnp.dot(
+                pick[i * tall:(i + 1) * tall], y_ref[:, k:k + wide], preferred_element_type=jnp.float32
             ).astype(jnp.bfloat16)
         stores.append(pltpu.make_async_copy(block.at[i], out_ref.at[i * tall:(i + 1) * tall], out_sem.at[i]))
         stores[i].start()
@@ -681,22 +655,16 @@
 
 def combine(place, y):
     tokens, width = place.shape[1], y.shape[1]
-    wide = 512 if width % 512 == 0 else width
     tall = CAP if tokens % CAP == 0 else tokens
-    count, steps = width // wide, tokens // tall
-    any_spec = pl.BlockSpec(memory_space=pl.ANY)
-    dma = pltpu.SemaphoreType.DMA
+    steps = tokens // tall
+    vmem = pl.BlockSpec(memory_space=pltpu.VMEM)
     return pl.pallas_call(
         combine_kernel,
         out_shape=jax.ShapeDtypeStruct((tokens, width), jnp.bfloat16),
-        in_specs=[any_spec, any_spec],
-        out_specs=any_spec,
-        scratch_shapes=[
-            pltpu.VMEM((1, tokens), jnp.int32),
-            pltpu.VMEM((count, CAP, wide), jnp.bfloat16),
-            pltpu.VMEM((steps, tall, width), jnp.bfloat16),
-            dma((count + 1,)), dma((steps,)),
-        ],
+        in_specs=[vmem, vmem],
+        out_specs=pl.BlockSpec(memory_space=pl.ANY),
+        scratch_shapes=[pltpu.VMEM((steps, tall, width), jnp.bfloat16), pltpu.SemaphoreType.DMA((steps,))],
+        compiler_params=pltpu.CompilerParams(vmem_limit_bytes=32 * 1024 * 1024),
     )(place, y)
 
 

time: 77.6 us -> 75.8 us (0.977)
  Pallas kernels: 77.3 us -> 75.5 us
    pallas_call x1, Pallas kernels: 3.5 us -> 2.4 us  [combine(): pl.pallas_call(combine_kernel, out_shape=jax.ShapeDtypeStruct((tokens, wi...]
where the time goes in v7:
time: 75.8 us; the launch traced here: 75.5 us
  Pallas kernels  75.5 us (100%)
    pallas_call x1, Pallas kernels, expert(): pl.pallas_call(functools.partial(expert_kernel, n), out_shape=(pltpu.VMEM...  73.1 us
    pallas_call x1, Pallas kernels, combine(): pl.pallas_call(combine_kernel, out_shape=jax.ShapeDtypeStruct((tokens, wi...  2.4 us

profile of v7, /device:TPU:3, one launch (start us, length us, event | category | flops | bytes accessed | tf_op | source)
XLA Modules:
  0.0 75.5 jit_solution(15249206973971164234)
XLA Ops:
  0.0 73.1 %shard_map.73 = (bf16[128,2048]{1,0:T(8,128)(2,1)S(1)}, s32[1,1024]{1,0:T(1,128)S(1)}) custom-call(s32[8,1024]{1,0:T(8,128)} %bitcast.3, s32[8,1024]{1,0:T(8,128)} %bitcast.4, f32[8,1024]{1,0:T(8,128)} %bitcast.5, bf16[1024,4096]{1,0:T(8,128)(2,1)} %tok_ref.1, bf16[256,768]{1,0:T(8,128)(2,1)} %gate_ref.1, bf16[256,768]{1,0:T(8,128)(2,1)} %up_ref.1, ...), custom_call_target="tpu_custom_call" | custom-call | tf_op jit(solution)/shard_map/pallas_call | solution.py:591
  73.1 2.4 %shard_map.74 = bf16[1024,2048]{1,0:T(8,128)(2,1)} custom-call(s32[1,1024]{1,0:T(1,128)S(1)} %get-tuple-element.7.place_ref, bf16[128,2048]{1,0:T(8,128)(2,1)S(1)} %get-tuple-element.8.y_ref), custom_call_target="tpu_custom_call" | custom-call | tf_op jit(solution)/shard_map/pallas_call | solution.py:661

commit v8 on v7

--- a/solution.py
+++ b/solution.py
@@ -14,7 +14,7 @@
 def expert_kernel(
     n,
     ids_ref, keep_ref, route_ref, tok_ref, gate_ref, up_ref, down_ref,
-    y_ref, place_ref,
+    y_ref, pick_ref,
     ids, keep, weight, w1, w2, stage, tok_buf, guest_out, own_rows, guest_rows, own_acc, part_out, part_in, hidden,
     x_own, x_out, x_in, y_own, y_out, y_in, xy_own, xy_out, xy_in, yx_out, yx_in, count, counts, route,
     load_sem, tok_sem, c_sem, e_send, l1_send, l1_recv, b1_send, b1_recv, l2_send, l2_recv, b2_send, b2_recv,
@@ -247,7 +247,6 @@
         running = running + jnp.where(lane >= shift, pltpu.roll(running, shift, 1), 0)
         shift *= 2
     place = jnp.where(chosen == 1, running[0:1] - 1, -1)
-    place_ref[...] = place
     count[...] = jnp.broadcast_to(jnp.sum(chosen, axis=1, keepdims=True), count.shape)
     slot_ids = lax.broadcasted_iota(jnp.int32, (CAP, length), 0)
     hit = place == slot_ids
@@ -268,6 +267,8 @@
         own_rows[i, y] = jnp.dot(
             table, tok_buf[sub + i], preferred_element_type=jnp.float32
         ).astype(jnp.bfloat16)
+
+    pick_ref[...] = table.T
 
     @pl.loop(1, n)
     def _(k):
@@ -591,7 +592,7 @@
     return pl.pallas_call(
         functools.partial(expert_kernel, n),
         out_shape=(
-            pltpu.VMEM((CAP, span * group), bf16), pltpu.VMEM((1, tokens.shape[0]), jnp.int32)
+            pltpu.VMEM((CAP, span * group), bf16), pltpu.VMEM((tokens.shape[0], CAP), bf16)
         ),
         in_specs=[any_spec] * 7,
         out_specs=(vmem, vmem),
@@ -636,16 +637,14 @@
     )(ids, keep, weight, tokens, gate, up, down)
 
 
-def combine_kernel(place_ref, y_ref, out_ref, block, out_sem):
+def combine_kernel(pick_ref, y_ref, out_ref, block, out_sem):
     steps, tall, width = block.shape
     wide = 512 if width % 512 == 0 else width
-    slots = lax.broadcasted_iota(jnp.int32, (CAP, steps * tall), 0)
-    pick = jnp.where(place_ref[...] == slots, jnp.float32(1.0), jnp.float32(0.0)).astype(jnp.bfloat16).T
     stores = []
     for i in range(steps):
         for k in range(0, width, wide):
             block[i, :, k:k + wide] = jnp.dot(
-                pick[i * tall:(i + 1) * tall], y_ref[:, k:k + wide], preferred_element_type=jnp.float32
+                pick_ref[i * tall:(i + 1) * tall], y_ref[:, k:k + wide], preferred_element_type=jnp.float32
             ).astype(jnp.bfloat16)
         stores.append(pltpu.make_async_copy(block.at[i], out_ref.at[i * tall:(i + 1) * tall], out_sem.at[i]))
         stores[i].start()
@@ -653,8 +652,8 @@
         store.wait()
 
 
-def combine(place, y):
-    tokens, width = place.shape[1], y.shape[1]
+def combine(pick, y):
+    tokens, width = pick.shape[0], y.shape[1]
     tall = CAP if tokens % CAP == 0 else tokens
     steps = tokens // tall
     vmem = pl.BlockSpec(memory_space=pltpu.VMEM)
@@ -665,12 +664,12 @@
         out_specs=pl.BlockSpec(memory_space=pl.ANY),
         scratch_shapes=[pltpu.VMEM((steps, tall, width), jnp.bfloat16), pltpu.SemaphoreType.DMA((steps,))],
         compiler_params=pltpu.CompilerParams(vmem_limit_bytes=32 * 1024 * 1024),
-    )(place, y)
+    )(pick, y)
 
 
 def per_device(tokens, expert_ids, keep_mask, route_weight, gate_weight, up_weight, down_weight):
-    y, place = expert(expert_ids.T, keep_mask.T, route_weight.T, tokens, gate_weight, up_weight, down_weight)
-    return combine(place, y)
+    y, pick = expert(expert_ids.T, keep_mask.T, route_weight.T, tokens, gate_weight, up_weight, down_weight)
+    return combine(pick, y)
 
 
 def solution(mesh):

time: 75.8 us -> 75.8 us (level)
  no operation moved by 1% of the time
where the time goes in v8:
time: 75.8 us; the launch traced here: 75.5 us
  Pallas kernels  75.4 us (99%)
    pallas_call x1, Pallas kernels, expert(): pl.pallas_call(functools.partial(expert_kernel, n), out_shape=(pltpu.VMEM...  73.1 us
    pallas_call x1, Pallas kernels, combine(): pl.pallas_call(combine_kernel, out_shape=jax.ShapeDtypeStruct((tokens, wi...  2.36 us

profile of v8, /device:TPU:3, one launch (start us, length us, event | category | flops | bytes accessed | tf_op | source)
XLA Modules:
  0.0 75.5 jit_solution(14220819327415046263)
XLA Ops:
  0.0 73.1 %shard_map.73 = (bf16[128,2048]{1,0:T(8,128)(2,1)S(1)}, bf16[1024,128]{1,0:T(8,128)(2,1)S(1)}) custom-call(s32[8,1024]{1,0:T(8,128)} %bitcast.3, s32[8,1024]{1,0:T(8,128)} %bitcast.4, f32[8,1024]{1,0:T(8,128)} %bitcast.5, bf16[1024,4096]{1,0:T(8,128)(2,1)} %tok_ref.1, bf16[256,768]{1,0:T(8,128)(2,1)} %gate_ref.1, bf16[256,768]{1,0:T(8,128)(2,1)} %up_ref.1, ...), custom_call_target="tpu_custom_call" | custom-call | tf_op jit(solution)/shard_map/pallas_call | solution.py:592
  73.1 2.4 %shard_map.74 = bf16[1024,2048]{1,0:T(8,128)(2,1)} custom-call(bf16[1024,128]{1,0:T(8,128)(2,1)S(1)} %get-tuple-element.7.pick_ref, bf16[128,2048]{1,0:T(8,128)(2,1)S(1)} %get-tuple-element.8.y_ref), custom_call_target="tpu_custom_call" | custom-call | tf_op jit(solution)/shard_map/pallas_call | solution.py:660
